TPU v7x, 32 devices: a whole 2x2x4 slice. The times are simulated.
32 devices in a mesh: groups: 2 (over x), seq: 16 (over z, y, core).
Axes of the slice: x: 2, y: 2, z: 4, core: 2. Of those that a mesh axis runs over, the one named last changes fastest.
Arguments:
- first_queries: bfloat16 [4096, 2048], P(('groups', 'seq')), parts along dimension 0, may hold values from -12 to 12
- second_queries: bfloat16 [4096, 2048], P(('groups', 'seq')), parts along dimension 0, may hold values from -12 to 12
- common_keys: bfloat16 [4096, 512], P(('groups', 'seq')), parts along dimension 0, may hold values from -4 to 4
- common_values: bfloat16 [4096, 512], P(('groups', 'seq')), parts along dimension 0, may hold values from -6 to 6
- lengths: int32 [8], P('groups'), parts along dimension 0, may hold values from 1 to 1024, 2048 in all
Outputs:
- first_output: bfloat16 [4096, 2048], P(('groups', 'seq')), parts along dimension 0
- second_output: bfloat16 [4096, 2048], P(('groups', 'seq')), parts along dimension 0
There are 2 independent parts, one for each index of `groups`. A program takes and returns all parts, laid end to end along the dimension named above; each array names one. Nothing has to cross between parts.
Inputs may be any that keep to these rules, and one draw needn't show every extreme that they name: `lengths`: the 4 documents lie end to end in order and fill all 2048 positions.
All inputs are finite; a program needn't handle non-finite values.
Results may differ from a plain program's by a relative error of at most 0.0034.
Values may be sent and summed in bfloat16 or wider, within the bound.
No kernel may reach another device: no remote copies, remote signals or barrier semaphores. Data moves between devices by JAX's collectives and lax.ppermute only.
A program may use at most 64 MiB of HBM per device.

v0:
```python
import jax
import jax.numpy as jnp
from jax import lax
from jax.sharding import PartitionSpec as P

HEAD_WIDTH = 128
QUERY_HEAD_COUNT = 16
KEY_VALUE_HEADS = 4


def from_partner(block, axis, distance):
    count = lax.axis_size(axis)
    route = []
    for low in range(count):
        high = low | 1 << distance
        if high != low and high < count:
            route += [(low, high), (high, low)]
    return lax.ppermute(block, axis, route)


def document_of(places, lengths):
    bounds = jnp.cumsum(lengths)
    return jnp.sum((places[:, None] >= bounds[None, :-1]).astype(jnp.int32), axis=1)


def attend(queries, query_places, all_keys, all_values, key_places, lengths):
    query_rows, head_size = queries.shape
    key_rows = all_keys.shape[0]
    query_block = min(1024, query_rows)
    key_block = min(2048, key_rows)
    score_scale = head_size ** (-0.5)
    query_document = document_of(query_places, lengths)
    key_document = document_of(key_places, lengths)
    key_tiles = (
        all_keys.reshape(-1, key_block, head_size),
        all_values.reshape(-1, key_block, head_size),
        key_places.reshape(-1, key_block),
        key_document.reshape(-1, key_block),
    )

    def one_tile(inputs):
        query_tile, tile_places, tile_document = inputs

        def absorb(carried, key_tile):
            running_max, running_sum, weighted = carried
            tile_keys, tile_values, tile_key_places, tile_key_document = key_tile
            scores = (
                jnp.einsum("qd,kd->qk", query_tile, tile_keys, preferred_element_type=jnp.float32)
                * score_scale
            )
            visible = (tile_key_places[None, :] <= tile_places[:, None]) & (
                tile_key_document[None, :] == tile_document[:, None]
            )
            masked = jnp.where(visible, scores, -1e30)
            new_max = jnp.maximum(running_max, jnp.max(masked, axis=1))
            weights = jnp.where(visible, jnp.exp(masked - new_max[:, None]), 0.0)
            factor = jnp.exp(running_max - new_max)
            new_sum = running_sum * factor + jnp.sum(weights, axis=1)
            product = jnp.dot(
                weights.astype(jnp.bfloat16), tile_values, preferred_element_type=jnp.float32
            )
            return (new_max, new_sum, weighted * factor[:, None] + product)

        def keep_carried(carried, key_tile):
            return carried

        def advance(carried, key_tile):
            tile_keys, tile_values, tile_key_places, tile_key_document = key_tile
            needed = (
                (jnp.min(tile_key_places) <= jnp.max(tile_places))
                & (jnp.min(tile_key_document) <= jnp.max(tile_document))
                & (jnp.max(tile_key_document) >= jnp.min(tile_document))
            )
            return (lax.cond(needed, absorb, keep_carried, carried, key_tile), None)

        initial = (
            jnp.full((query_block,), -1e30, jnp.float32),
            jnp.zeros((query_block,), jnp.float32),
            jnp.zeros((query_block, head_size), jnp.float32),
        )
        finished, unused = lax.scan(advance, initial, key_tiles)
        return (finished[2] / finished[1][:, None]).astype(jnp.bfloat16)

    blended = lax.map(
        one_tile,
        (
            queries.reshape(-1, query_block, head_size),
            query_places.reshape(-1, query_block),
            query_document.reshape(-1, query_block),
        ),
    )
    return blended.reshape(query_rows, head_size)


def on_device(first_queries, second_queries, common_keys, common_values, lengths):
    members = lax.axis_size("seq")
    device = lax.axis_index("seq")
    token_total = common_keys.shape[0]
    heads_per_group = max(QUERY_HEAD_COUNT // members, 1)
    phase_angles = max(members // QUERY_HEAD_COUNT, 1)
    head_groups = QUERY_HEAD_COUNT // heads_per_group
    head_fraction = QUERY_HEAD_COUNT // KEY_VALUE_HEADS // heads_per_group
    key_sharers = members // KEY_VALUE_HEADS
    slot_rows = token_total // phase_angles
    own_phase = device // head_groups
    arrived_rows = members * slot_rows
    flat_rows = jnp.arange(arrived_rows, dtype=jnp.int32)
    query_places = (
        flat_rows // slot_rows * token_total + flat_rows % slot_rows * phase_angles + own_phase
    )
    query_places = jnp.tile(query_places, heads_per_group)
    piece_rows = token_total // key_sharers

    def thin_slots(source_tensor):
        return (
            source_tensor.reshape(
                piece_rows, phase_angles, head_fraction, KEY_VALUE_HEADS, HEAD_WIDTH
            )
            .transpose(0, 1, 3, 2, 4)
            .reshape(piece_rows, members, HEAD_WIDTH)
        )

    arrived_keys, arrived_values = (
        lax.all_to_all(thin_slots(common_keys), "seq", split_axis=1, concat_axis=0, tiled=True),
        lax.all_to_all(thin_slots(common_values), "seq", split_axis=1, concat_axis=0, tiled=True),
    )
    own_piece = own_phase * head_fraction + device % head_fraction
    stacked_keys = arrived_keys.reshape(1, members * piece_rows, HEAD_WIDTH)
    stacked_values = arrived_values.reshape(1, members * piece_rows, HEAD_WIDTH)
    low_bits = head_fraction.bit_length() - 1
    skipped = head_groups.bit_length() - 1
    for section_index in range(key_sharers.bit_length() - 1):
        partner_bit = (
            section_index if section_index < low_bits else section_index - low_bits + skipped
        )
        other_keys, other_values = from_partner((stacked_keys, stacked_values), "seq", partner_bit)
        is_upper = own_piece >> section_index & 1 == 1
        stacked_keys = jnp.concatenate(
            [
                jnp.where(is_upper, other_keys, stacked_keys),
                jnp.where(is_upper, stacked_keys, other_keys),
            ],
            axis=0,
        )
        stacked_values = jnp.concatenate(
            [
                jnp.where(is_upper, other_values, stacked_values),
                jnp.where(is_upper, stacked_values, other_values),
            ],
            axis=0,
        )
    all_keys = stacked_keys.transpose(1, 0, 2).reshape(-1, HEAD_WIDTH)
    all_values = stacked_values.transpose(1, 0, 2).reshape(-1, HEAD_WIDTH)
    key_places = jnp.arange(members * token_total, dtype=jnp.int32)

    def attend_layer(queries):
        outgoing = queries.reshape(slot_rows, members, heads_per_group * HEAD_WIDTH)
        arrived = lax.all_to_all(outgoing, "seq", split_axis=1, concat_axis=0, tiled=True)
        query_rows = arrived.transpose(1, 0, 2).reshape(-1, HEAD_WIDTH)
        blended = attend(query_rows, query_places, all_keys, all_values, key_places, lengths)
        results = blended.reshape(heads_per_group, arrived_rows, HEAD_WIDTH).transpose(1, 0, 2)
        returned = lax.all_to_all(results, "seq", split_axis=0, concat_axis=1, tiled=True)
        return returned.reshape(token_total, QUERY_HEAD_COUNT * HEAD_WIDTH)

    return (attend_layer(first_queries), attend_layer(second_queries))


def solution(mesh):
    in_specs = (
        P(("groups", "seq"), None),
        P(("groups", "seq"), None),
        P(("groups", "seq"), None),
        P(("groups", "seq"), None),
        P("groups"),
    )
    out_specs = (P(("groups", "seq"), None), P(("groups", "seq"), None))
    return jax.shard_map(
        on_device, mesh=mesh, in_specs=in_specs, out_specs=out_specs, check_vma=False
    )
```

profile of v0, /device:TPU:0, one launch (start us, length us, event | category | flops | bytes accessed | tf_op | source)
XLA Modules:
  0.0 141.1 jit_solution(11742205075738446367)
XLA Ops:
  2.3 7.4 %all-to-all-start.1 = ((bf16[32,16,128]{2,0,1:T(8,128)(2,1)}), bf16[32,16,128]{2,0,1:T(8,128)(2,1)S(1)}, u32[]{:S(2)}, u32[]{:S(2)}) async-start(bf16[32,16,128]{2,0,1:T(8,128)(2,1)} %bitcast.21), calls=%async_computation.1 | async-start | bytes 262144 | tf_op jit(solution)/shard_map/all_to_all | solution.py:124
  13.1 4.5 %all-to-all-done.1 = bf16[32,16,128]{2,0,1:T(8,128)(2,1)S(1)} async-done(((bf16[32,16,128]{2,0,1:T(8,128)(2,1)}), bf16[32,16,128]{2,0,1:T(8,128)(2,1)S(1)}, u32[]{:S(2)}, u32[]{:S(2)}) %all-to-all-start.1) | async-done | bytes 131104 | tf_op jit(solution)/shard_map/all_to_all | solution.py:124
  17.7 3.5 %all-to-all-start.2 = ((bf16[32,16,128]{2,0,1:T(8,128)(2,1)}), bf16[32,16,128]{2,0,1:T(8,128)(2,1)S(1)}, u32[]{:S(2)}, u32[]{:S(2)}) async-start(bf16[32,16,128]{2,0,1:T(8,128)(2,1)} %bitcast.30), calls=%async_computation.2 | async-start | bytes 262144 | tf_op jit(solution)/shard_map/all_to_all | solution.py:125
  21.2 2.0 %copy_bitcast_fusion.1 = bf16[128,16,128]{2,0,1:T(8,128)(2,1)} fusion(bf16[128,2048]{1,0:T(8,128)(2,1)} %param.13), kind=kLoop, calls=%fused_computation.51 | loop fusion | bytes 1048576 | tf_op jit(solution)/shard_map/reshape | solution.py:157
  23.4 5.6 %all-to-all-done.2 = bf16[32,16,128]{2,0,1:T(8,128)(2,1)S(1)} async-done(((bf16[32,16,128]{2,0,1:T(8,128)(2,1)}), bf16[32,16,128]{2,0,1:T(8,128)(2,1)S(1)}, u32[]{:S(2)}, u32[]{:S(2)}) %all-to-all-start.2) | async-done | bytes 131104 | tf_op jit(solution)/shard_map/all_to_all | solution.py:125
  29.0 3.6 %all-to-all-start.4 = ((bf16[128,16,128]{2,0,1:T(8,128)(2,1)}), bf16[128,16,128]{2,0,1:T(8,128)(2,1)S(1)}, u32[]{:S(2)}, u32[]{:S(2)}) async-start(bf16[128,16,128]{2,0,1:T(8,128)(2,1)} %copy_bitcast_fusion), calls=%async_computation.4 | async-start | bytes 1048576 | tf_op jit(solution)/shard_map/all_to_all | solution.py:158
  34.2 1.8 %collective-permute-start.3 = (bf16[2,512,128]{2,1,0:T(8,128)(2,1)S(1)}, bf16[2,512,128]{2,1,0:T(8,128)(2,1)S(1)}, u32[]{:S(2)}, u32[]{:S(2)}) collective-permute-start(bf16[2,512,128]{2,1,0:T(8,128)(2,1)S(1)} %pad_maximum_fusion.1), channel_id=1, source_target_pairs={{0,2},{2,0},{1,3},{3,1},{4,6},{6,4},{5,7},{7,5},{8,10},{10,8},{9,1... | collective-permute-start | bytes 786440 | tf_op jit(solution)/shard_map/ppermute | solution.py:18
  37.1 10.0 %collective-permute-done.3 = bf16[2,512,128]{2,1,0:T(8,128)(2,1)S(1)} collective-permute-done((bf16[2,512,128]{2,1,0:T(8,128)(2,1)S(1)}, bf16[2,512,128]{2,1,0:T(8,128)(2,1)S(1)}, u32[]{:S(2)}, u32[]{:S(2)}) %collective-permute-start.3) | collective-permute-done | bytes 262176 | tf_op jit(solution)/shard_map/ppermute | solution.py:18
  47.6 5.2 %all-to-all-start = ((bf16[128,16,128]{2,0,1:T(8,128)(2,1)}), bf16[128,16,128]{2,0,1:T(8,128)(2,1)S(1)}, u32[]{:S(2)}, u32[]{:S(2)}) async-start(bf16[128,16,128]{2,0,1:T(8,128)(2,1)} %copy_bitcast_fusion.1), calls=%async_computation | async-start | bytes 1048576 | tf_op jit(solution)/shard_map/all_to_all | solution.py:158
  52.9 1.2 copy.45
  54.2 27.1 %while.51 = (s32[]{:T(128)}, bf16[2,1024,128]{2,1,0:T(8,128)(2,1)S(1)}, s32[2,1024]{1,0:T(2,128)S(1)}, s32[2,1024]{1,0:T(2,128)S(1)}, s32[]{:T(128)}, /*index=5*...) while((s32[]{:T(128)}, ...), condition=%wide.region_22.23_spmd.clone, body=%wide.region_14.22_spmd.clone.sunk | while | flops 1120409600 | bytes 28991804 | solution.py:84
  58.1 9.3 %conditional.7 = ((f32[1024]{0:T(1024)S(1)}, f32[1024,128]{1,0:T(8,128)S(1)})) conditional(s32[]{:T(128)} %convert_element_type.75, (f32[1024]{0:T(1024)S(1)}, f32[1024,128]{1,0:T(8,128)S(1)}) %tuple.143, (s32[1,2048]{1,0:T(1,128)S(1)}, s32[1,1024]{1,0:T(1,128)S(1)}, s32[1,2048]{1,0:T(1,128)S(1)}, s32[1,1024]{1,0:T(1,128)S(1)}, ...), branch_computations={%region_18.18_spmd, %region_19.21_spmd} | conditional | flops 1120144384 | bytes 27648028 | solution.py:74
  58.1 3.5 %fusion.21 = (f32[1024]{0:T(1024)S(1)}, f32[1024,2048]{1,0:T(8,128)S(1)}) fusion(s32[2048]{0:T(1024)S(1)} %bitcast.107, s32[2048]{0:T(1024)S(1)} %bitcast.113, s32[1024]{0:T(1024)S(1)} %bitcast.126, s32[1024]{0:T(1024)S(1)} %bitcast.129, bf16[1,2048,128]{2,1,0:T(8,128)(2,1)} %get-tuple-element.513, bf16[2,1024,128]{2,1,0:T(8,128)(2,1)S(1)} %get-tuple-element.511, ...), kind=kOutput, calls=%fused_computation.25 | convolution fusion | flops 549452800 | bytes 9203716 | tf_op jit(solution)/shard_map/while/body/eval_jaxpr/while/body/eval_jaxpr/cond/branch_1_fun/qd,kd->qk/dot_general | solution.py:48
  61.7 3.2 %fusion.23 = f32[1024]{0:T(1024)S(1)} fusion(f32[1024,2048]{1,0:T(8,128)S(1)} %get-tuple-element.653, f32[1024]{0:T(1024)S(1)} %broadcast_maximum_fusion.1, s32[2048]{0:T(1024)S(1)} %bitcast.108, s32[2048]{0:T(1024)S(1)} %bitcast.114, s32[1024]{0:T(1024)S(1)} %bitcast.127, s32[1024]{0:T(1024)S(1)} %bitcast.130), kind=kLoop, calls=%fused_computation.27 | loop fusion | flops 16776192 | bytes 8421376 | tf_op jit(solution)/shard_map/while/body/eval_jaxpr/while/body/eval_jaxpr/cond/branch_1_fun/reduce_sum | solution.py:58
  64.9 2.6 %fusion.26 = f32[1024,128]{1,0:T(8,128)S(1)} fusion(f32[1024,2048]{1,0:T(8,128)S(1)} %get-tuple-element.653, f32[1024]{0:T(1024)S(1)} %broadcast_maximum_fusion.1, s32[2048]{0:T(1024)S(1)} %bitcast.109, s32[2048]{0:T(1024)S(1)} %bitcast.115, s32[1024]{0:T(1024)S(1)} %bitcast.128, s32[1024]{0:T(1024)S(1)} %bitcast.131, ...), kind=kOutput, calls=%fused_computation.29 | convolution fusion | flops 553910272 | bytes 9994240 | tf_op jit(solution)/shard_map/while/body/eval_jaxpr/while/body/eval_jaxpr/cond/branch_1_fun/dot_general | solution.py:59
  71.7 9.3 %conditional.7 = ((f32[1024]{0:T(1024)S(1)}, f32[1024,128]{1,0:T(8,128)S(1)})) conditional(s32[]{:T(128)} %convert_element_type.75, (f32[1024]{0:T(1024)S(1)}, f32[1024,128]{1,0:T(8,128)S(1)}) %tuple.143, (s32[1,2048]{1,0:T(1,128)S(1)}, s32[1,1024]{1,0:T(1,128)S(1)}, s32[1,2048]{1,0:T(1,128)S(1)}, s32[1,1024]{1,0:T(1,128)S(1)}, ...), branch_computations={%region_18.18_spmd, %region_19.21_spmd} | conditional | flops 1120144384 | bytes 27648028 | solution.py:74
  71.7 3.5 %fusion.21 = (f32[1024]{0:T(1024)S(1)}, f32[1024,2048]{1,0:T(8,128)S(1)}) fusion(s32[2048]{0:T(1024)S(1)} %bitcast.107, s32[2048]{0:T(1024)S(1)} %bitcast.113, s32[1024]{0:T(1024)S(1)} %bitcast.126, s32[1024]{0:T(1024)S(1)} %bitcast.129, bf16[1,2048,128]{2,1,0:T(8,128)(2,1)} %get-tuple-element.513, bf16[2,1024,128]{2,1,0:T(8,128)(2,1)S(1)} %get-tuple-element.511, ...), kind=kOutput, calls=%fused_computation.25 | convolution fusion | flops 549452800 | bytes 9203716 | tf_op jit(solution)/shard_map/while/body/eval_jaxpr/while/body/eval_jaxpr/cond/branch_1_fun/qd,kd->qk/dot_general | solution.py:48
  75.2 3.2 %fusion.23 = f32[1024]{0:T(1024)S(1)} fusion(f32[1024,2048]{1,0:T(8,128)S(1)} %get-tuple-element.653, f32[1024]{0:T(1024)S(1)} %broadcast_maximum_fusion.1, s32[2048]{0:T(1024)S(1)} %bitcast.108, s32[2048]{0:T(1024)S(1)} %bitcast.114, s32[1024]{0:T(1024)S(1)} %bitcast.127, s32[1024]{0:T(1024)S(1)} %bitcast.130), kind=kLoop, calls=%fused_computation.27 | loop fusion | flops 16776192 | bytes 8421376 | tf_op jit(solution)/shard_map/while/body/eval_jaxpr/while/body/eval_jaxpr/cond/branch_1_fun/reduce_sum | solution.py:58
  78.4 2.6 %fusion.26 = f32[1024,128]{1,0:T(8,128)S(1)} fusion(f32[1024,2048]{1,0:T(8,128)S(1)} %get-tuple-element.653, f32[1024]{0:T(1024)S(1)} %broadcast_maximum_fusion.1, s32[2048]{0:T(1024)S(1)} %bitcast.109, s32[2048]{0:T(1024)S(1)} %bitcast.115, s32[1024]{0:T(1024)S(1)} %bitcast.128, s32[1024]{0:T(1024)S(1)} %bitcast.131, ...), kind=kOutput, calls=%fused_computation.29 | convolution fusion | flops 553910272 | bytes 9994240 | tf_op jit(solution)/shard_map/while/body/eval_jaxpr/while/body/eval_jaxpr/cond/branch_1_fun/dot_general | solution.py:59
  83.8 6.0 %all-to-all-start.5 = ((bf16[16,2,8192]{2,1,0:T(2,128)(2,1)}), bf16[16,2,8192]{2,1,0:T(2,128)(2,1)S(1)}, u32[]{:S(2)}, u32[]{:S(2)}) async-start(bf16[16,2,8192]{2,1,0:T(2,128)(2,1)} %reshape.117), calls=%async_computation.5 | async-start | bytes 1048576 | tf_op jit(solution)/shard_map/all_to_all | solution.py:162
  89.9 27.1 %while.50 = (s32[]{:T(128)}, bf16[2,1024,128]{2,1,0:T(8,128)(2,1)S(1)}, s32[2,1024]{1,0:T(2,128)S(1)}, s32[2,1024]{1,0:T(2,128)S(1)}, s32[]{:T(128)}, /*index=5*...) while((s32[]{:T(128)}, ...), condition=%wide.region_13.14_spmd.clone, body=%wide.region_5.13_spmd.clone.sunk | while | flops 1120409600 | bytes 28991804 | solution.py:84
  93.8 9.3 %conditional.6 = ((f32[1024]{0:T(1024)S(1)}, f32[1024,128]{1,0:T(8,128)S(1)})) conditional(s32[]{:T(128)} %convert_element_type.73, (f32[1024]{0:T(1024)S(1)}, f32[1024,128]{1,0:T(8,128)S(1)}) %tuple.139, (s32[1,2048]{1,0:T(1,128)S(1)}, s32[1,1024]{1,0:T(1,128)S(1)}, s32[1,2048]{1,0:T(1,128)S(1)}, s32[1,1024]{1,0:T(1,128)S(1)}, ...), branch_computations={%region_9.9_spmd, %region_10.12_spmd} | conditional | flops 1120144384 | bytes 27648028 | solution.py:74
  93.8 3.5 %fusion.4 = (f32[1024]{0:T(1024)S(1)}, f32[1024,2048]{1,0:T(8,128)S(1)}) fusion(s32[2048]{0:T(1024)S(1)} %bitcast.110, s32[2048]{0:T(1024)S(1)} %bitcast.116, s32[1024]{0:T(1024)S(1)} %bitcast.132, s32[1024]{0:T(1024)S(1)} %bitcast.135, bf16[1,2048,128]{2,1,0:T(8,128)(2,1)} %get-tuple-element.489, bf16[2,1024,128]{2,1,0:T(8,128)(2,1)S(1)} %get-tuple-element.487, ...), kind=kOutput, calls=%fused_computation.5 | convolution fusion | flops 549452800 | bytes 9203716 | tf_op jit(solution)/shard_map/while/body/eval_jaxpr/while/body/eval_jaxpr/cond/branch_1_fun/qd,kd->qk/dot_general | solution.py:48
  97.3 3.2 %fusion.6 = f32[1024]{0:T(1024)S(1)} fusion(f32[1024,2048]{1,0:T(8,128)S(1)} %get-tuple-element.649, f32[1024]{0:T(1024)S(1)} %broadcast_maximum_fusion, s32[2048]{0:T(1024)S(1)} %bitcast.111, s32[2048]{0:T(1024)S(1)} %bitcast.117, s32[1024]{0:T(1024)S(1)} %bitcast.133, s32[1024]{0:T(1024)S(1)} %bitcast.136), kind=kLoop, calls=%fused_computation.7 | loop fusion | flops 16776192 | bytes 8421376 | tf_op jit(solution)/shard_map/while/body/eval_jaxpr/while/body/eval_jaxpr/cond/branch_1_fun/reduce_sum | solution.py:58
  100.6 2.6 %fusion.9 = f32[1024,128]{1,0:T(8,128)S(1)} fusion(f32[1024,2048]{1,0:T(8,128)S(1)} %get-tuple-element.649, f32[1024]{0:T(1024)S(1)} %broadcast_maximum_fusion, s32[2048]{0:T(1024)S(1)} %bitcast.112, s32[2048]{0:T(1024)S(1)} %bitcast.118, s32[1024]{0:T(1024)S(1)} %bitcast.134, s32[1024]{0:T(1024)S(1)} %bitcast.137, ...), kind=kOutput, calls=%fused_computation.9 | convolution fusion | flops 553910272 | bytes 9994240 | tf_op jit(solution)/shard_map/while/body/eval_jaxpr/while/body/eval_jaxpr/cond/branch_1_fun/dot_general | solution.py:59
  107.4 9.3 %conditional.6 = ((f32[1024]{0:T(1024)S(1)}, f32[1024,128]{1,0:T(8,128)S(1)})) conditional(s32[]{:T(128)} %convert_element_type.73, (f32[1024]{0:T(1024)S(1)}, f32[1024,128]{1,0:T(8,128)S(1)}) %tuple.139, (s32[1,2048]{1,0:T(1,128)S(1)}, s32[1,1024]{1,0:T(1,128)S(1)}, s32[1,2048]{1,0:T(1,128)S(1)}, s32[1,1024]{1,0:T(1,128)S(1)}, ...), branch_computations={%region_9.9_spmd, %region_10.12_spmd} | conditional | flops 1120144384 | bytes 27648028 | solution.py:74
  107.4 3.5 %fusion.4 = (f32[1024]{0:T(1024)S(1)}, f32[1024,2048]{1,0:T(8,128)S(1)}) fusion(s32[2048]{0:T(1024)S(1)} %bitcast.110, s32[2048]{0:T(1024)S(1)} %bitcast.116, s32[1024]{0:T(1024)S(1)} %bitcast.132, s32[1024]{0:T(1024)S(1)} %bitcast.135, bf16[1,2048,128]{2,1,0:T(8,128)(2,1)} %get-tuple-element.489, bf16[2,1024,128]{2,1,0:T(8,128)(2,1)S(1)} %get-tuple-element.487, ...), kind=kOutput, calls=%fused_computation.5 | convolution fusion | flops 549452800 | bytes 9203716 | tf_op jit(solution)/shard_map/while/body/eval_jaxpr/while/body/eval_jaxpr/cond/branch_1_fun/qd,kd->qk/dot_general | solution.py:48
  110.9 3.2 %fusion.6 = f32[1024]{0:T(1024)S(1)} fusion(f32[1024,2048]{1,0:T(8,128)S(1)} %get-tuple-element.649, f32[1024]{0:T(1024)S(1)} %broadcast_maximum_fusion, s32[2048]{0:T(1024)S(1)} %bitcast.111, s32[2048]{0:T(1024)S(1)} %bitcast.117, s32[1024]{0:T(1024)S(1)} %bitcast.133, s32[1024]{0:T(1024)S(1)} %bitcast.136), kind=kLoop, calls=%fused_computation.7 | loop fusion | flops 16776192 | bytes 8421376 | tf_op jit(solution)/shard_map/while/body/eval_jaxpr/while/body/eval_jaxpr/cond/branch_1_fun/reduce_sum | solution.py:58
  114.1 2.6 %fusion.9 = f32[1024,128]{1,0:T(8,128)S(1)} fusion(f32[1024,2048]{1,0:T(8,128)S(1)} %get-tuple-element.649, f32[1024]{0:T(1024)S(1)} %broadcast_maximum_fusion, s32[2048]{0:T(1024)S(1)} %bitcast.112, s32[2048]{0:T(1024)S(1)} %bitcast.118, s32[1024]{0:T(1024)S(1)} %bitcast.134, s32[1024]{0:T(1024)S(1)} %bitcast.137, ...), kind=kOutput, calls=%fused_computation.9 | convolution fusion | flops 553910272 | bytes 9994240 | tf_op jit(solution)/shard_map/while/body/eval_jaxpr/while/body/eval_jaxpr/cond/branch_1_fun/dot_general | solution.py:59
  118.9 6.0 %all-to-all-start.3 = ((bf16[16,2,8192]{2,1,0:T(2,128)(2,1)}), bf16[16,2,8192]{2,1,0:T(2,128)(2,1)S(1)}, u32[]{:S(2)}, u32[]{:S(2)}) async-start(bf16[16,2,8192]{2,1,0:T(2,128)(2,1)} %reshape.115), calls=%async_computation.3 | async-start | bytes 1048576 | tf_op jit(solution)/shard_map/all_to_all | solution.py:162
  125.8 1.0 copy.54
  126.9 12.3 %all-to-all-done.3 = bf16[16,2,8192]{2,1,0:T(2,128)(2,1)S(1)} async-done(((bf16[16,2,8192]{2,1,0:T(2,128)(2,1)}), bf16[16,2,8192]{2,1,0:T(2,128)(2,1)S(1)}, u32[]{:S(2)}, u32[]{:S(2)}) %all-to-all-start.3) | async-done | bytes 524320 | tf_op jit(solution)/shard_map/all_to_all | solution.py:162
  (73 shorter events, 20.2 us)
Async XLA Ops:
  0.6 11.6 %copy-start = (bf16[128,2048]{1,0:T(8,128)(2,1)S(1)}, bf16[128,2048]{1,0:T(8,128)(2,1)}, u32[]{:S(2)}) copy-start(bf16[128,2048]{1,0:T(8,128)(2,1)} %param.14) | copy-start | bytes 1572868
  2.3 15.3 %all-to-all-start.1 = ((bf16[32,16,128]{2,0,1:T(8,128)(2,1)}), bf16[32,16,128]{2,0,1:T(8,128)(2,1)S(1)}, u32[]{:S(2)}, u32[]{:S(2)}) async-start(bf16[32,16,128]{2,0,1:T(8,128)(2,1)} %bitcast.21), calls=%async_computation.1 | async-start | bytes 262144 | tf_op jit(solution)/shard_map/all_to_all | solution.py:124
  17.7 11.4 %all-to-all-start.2 = ((bf16[32,16,128]{2,0,1:T(8,128)(2,1)}), bf16[32,16,128]{2,0,1:T(8,128)(2,1)S(1)}, u32[]{:S(2)}, u32[]{:S(2)}) async-start(bf16[32,16,128]{2,0,1:T(8,128)(2,1)} %bitcast.30), calls=%async_computation.2 | async-start | bytes 262144 | tf_op jit(solution)/shard_map/all_to_all | solution.py:125
  23.1 9.9 %collective-permute-start = (bf16[1,512,128]{2,1,0:T(8,128)(2,1)S(1)}, bf16[1,512,128]{2,1,0:T(8,128)(2,1)S(1)}, u32[]{:S(2)}, u32[]{:S(2)}) collective-permute-start(bf16[1,512,128]{2,1,0:T(8,128)(2,1)S(1)} %bitcast.124), channel_id=1, source_target_pairs={{0,1},{1,0},{2,3},{3,2},{4,5},{5,4},{6,7},{7,6},{8,9},{9,8},{10,11... | collective-permute-start | bytes 393224 | tf_op jit(solution)/shard_map/ppermute | solution.py:18
  29.0 18.6 %all-to-all-start.4 = ((bf16[128,16,128]{2,0,1:T(8,128)(2,1)}), bf16[128,16,128]{2,0,1:T(8,128)(2,1)S(1)}, u32[]{:S(2)}, u32[]{:S(2)}) async-start(bf16[128,16,128]{2,0,1:T(8,128)(2,1)} %copy_bitcast_fusion), calls=%async_computation.4 | async-start | bytes 1048576 | tf_op jit(solution)/shard_map/all_to_all | solution.py:158
  32.6 1.4 %collective-permute-start.2 = (bf16[1,512,128]{2,1,0:T(8,128)(2,1)S(1)}, bf16[1,512,128]{2,1,0:T(8,128)(2,1)S(1)}, u32[]{:S(2)}, u32[]{:S(2)}) collective-permute-start(bf16[1,512,128]{2,1,0:T(8,128)(2,1)S(1)} %bitcast.125), channel_id=1, source_target_pairs={{0,1},{1,0},{2,3},{3,2},{4,5},{5,4},{6,7},{7,6},{8,9},{9,8},{10,11... | collective-permute-start | bytes 393224 | tf_op jit(solution)/shard_map/ppermute | solution.py:18
  34.2 13.0 %collective-permute-start.3 = (bf16[2,512,128]{2,1,0:T(8,128)(2,1)S(1)}, bf16[2,512,128]{2,1,0:T(8,128)(2,1)S(1)}, u32[]{:S(2)}, u32[]{:S(2)}) collective-permute-start(bf16[2,512,128]{2,1,0:T(8,128)(2,1)S(1)} %pad_maximum_fusion.1), channel_id=1, source_target_pairs={{0,2},{2,0},{1,3},{3,1},{4,6},{6,4},{5,7},{7,5},{8,10},{10,8},{9,1... | collective-permute-start | bytes 786440 | tf_op jit(solution)/shard_map/ppermute | solution.py:18
  36.8 16.0 %collective-permute-start.1 = (bf16[2,512,128]{2,1,0:T(8,128)(2,1)S(1)}, bf16[2,512,128]{2,1,0:T(8,128)(2,1)S(1)}, u32[]{:S(2)}, u32[]{:S(2)}) collective-permute-start(bf16[2,512,128]{2,1,0:T(8,128)(2,1)S(1)} %pad_maximum_fusion), channel_id=1, source_target_pairs={{0,2},{2,0},{1,3},{3,1},{4,6},{6,4},{5,7},{7,5},{8,10},{10,8},{9,1... | collective-permute-start | bytes 786440 | tf_op jit(solution)/shard_map/ppermute | solution.py:18
  47.6 36.2 %all-to-all-start = ((bf16[128,16,128]{2,0,1:T(8,128)(2,1)}), bf16[128,16,128]{2,0,1:T(8,128)(2,1)S(1)}, u32[]{:S(2)}, u32[]{:S(2)}) async-start(bf16[128,16,128]{2,0,1:T(8,128)(2,1)} %copy_bitcast_fusion.1), calls=%async_computation | async-start | bytes 1048576 | tf_op jit(solution)/shard_map/all_to_all | solution.py:158
  83.8 35.1 %all-to-all-start.5 = ((bf16[16,2,8192]{2,1,0:T(2,128)(2,1)}), bf16[16,2,8192]{2,1,0:T(2,128)(2,1)S(1)}, u32[]{:S(2)}, u32[]{:S(2)}) async-start(bf16[16,2,8192]{2,1,0:T(2,128)(2,1)} %reshape.117), calls=%async_computation.5 | async-start | bytes 1048576 | tf_op jit(solution)/shard_map/all_to_all | solution.py:162
  118.9 20.3 %all-to-all-start.3 = ((bf16[16,2,8192]{2,1,0:T(2,128)(2,1)}), bf16[16,2,8192]{2,1,0:T(2,128)(2,1)S(1)}, u32[]{:S(2)}, u32[]{:S(2)}) async-start(bf16[16,2,8192]{2,1,0:T(2,128)(2,1)} %reshape.115), calls=%async_computation.3 | async-start | bytes 1048576 | tf_op jit(solution)/shard_map/all_to_all | solution.py:162
where the time goes:
time: 142 us; the launch traced here: 141 us
  starting transfers between devices  34.4 us (24%)
  waiting for transfers between devices  33.4 us (24%)
  matrix products  24.2 us (17%)
  other arithmetic  21.1 us (15%)
  local copies, waits for them, and re-layouts  14.4 us (10%)
  loops' own time  12.7 us (9%)
    dot_general x4, matrix products, absorb(): jnp.einsum('qd,kd->qk', query_tile, tile_keys, preferred_element_type=jnp...  13.9 us
    reduce_sum x4, other arithmetic, absorb(): new_sum = running_sum * factor + jnp.sum(weights, axis=1)  13 us
    another operation x2, loops' own time, attend(): lax.map(one_tile, (queries.reshape(-1, query_block, head_size), query_pla...  12.6 us
    all_to_all x2, waiting for transfers between devices, attend_layer(): lax.all_to_all(results, 'seq', split_axis=0, concat_axis=1, tiled=True)  12.3 us
    all_to_all x2, starting transfers between devices, attend_layer(): lax.all_to_all(results, 'seq', split_axis=0, concat_axis=1, tiled=True)  12 us
    ppermute x4, waiting for transfers between devices, from_partner(): return lax.ppermute(block, axis, route)  11 us
    dot_general x4, matrix products, absorb(): jnp.dot(weights.astype(jnp.bfloat16), tile_values, preferred_element_type...  10.2 us
    all_to_all x2, starting transfers between devices, attend_layer(): lax.all_to_all(outgoing, 'seq', split_axis=1, concat_axis=0, tiled=True)  8.74 us
  transfers between devices with their start and end apart: 10, of which 5 were waited for; matrix products, arithmetic and copies ran while one was open for 40% of the time, Pallas kernels for 0%

commit v1 on v0

v1 whole, which is shorter than its diff:
```python
import functools
import math

import jax
import jax.numpy as jnp
from jax import lax
from jax.experimental import pallas as pl
from jax.experimental.pallas import tpu as pltpu
from jax.sharding import PartitionSpec as P


HEAD_WIDTH = 128
QUERY_HEAD_COUNT = 16
KEY_VALUE_HEADS = 4

CORE = 1
ROW = 2
LEVEL = 4

HIDDEN = -1e30
NOWHERE = -(1 << 20)
PAIR = 2


def swapped(count, distance):
    return [(d, d ^ distance) for d in range(count)]


def shifted(count):
    return [(d, d + LEVEL) for d in range(count - LEVEL)]


def across(count):
    return [(d, d + LEVEL - ROW) for d in range(count - LEVEL) if d & ROW]


def pack_kernel(keys_ref, values_ref, packed_ref):
    for g in range(KEY_VALUE_HEADS):
        columns = pl.ds(g * HEAD_WIDTH, HEAD_WIDTH)
        packed_ref[g] = keys_ref[:, columns]
        packed_ref[KEY_VALUE_HEADS + g] = values_ref[:, columns].T


def pack(keys, values):
    tokens = keys.shape[0]
    return pl.pallas_call(
        pack_kernel,
        out_shape=jax.ShapeDtypeStruct((2 * KEY_VALUE_HEADS, tokens, HEAD_WIDTH), keys.dtype),
        name="pack",
    )(keys, values)


def attend_kernel(sources, count, first, last, *refs):
    refs = list(refs)
    device_ref, lengths_ref, first_ref, second_ref = refs[:4]
    blocks = refs[4 : 4 + count]
    rest = refs[4 + count :]
    if not first:
        sum_in, stat_in = rest[:2]
        rest = rest[2:]
    if last:
        out_refs, rest = rest[:2], rest[2:]
    else:
        sum_ref, stat_ref = rest[:2]
        rest = rest[2:]
    (bias_ref,) = rest
    if first:
        sum_in, stat_in = None, None

    tokens = first_ref.shape[0]
    device = device_ref[0]
    query_base = device * tokens
    bounds = []
    total = 0
    for k in range(lengths_ref.shape[0] - 1):
        total = total + lengths_ref[k]
        bounds.append(total)

    def start_of(place):
        start = jnp.zeros_like(place)
        for bound in bounds:
            start = jnp.where(place >= bound, bound, start)
        return start

    bases = []
    for source in sources:
        bases.append(source(device) * tokens)
    earliest = start_of(query_base)
    needed = functools.reduce(
        jnp.logical_or,
        [(b <= query_base + tokens - 1) & (b + tokens - 1 >= earliest) for b in bases],
    )

    group = QUERY_HEAD_COUNT // KEY_VALUE_HEADS
    pairs = group // PAIR
    steps = [(g, layer, pair) for g in range(KEY_VALUE_HEADS) for layer in range(2) for pair in range(pairs)]
    factor = math.log2(math.e) / math.sqrt(HEAD_WIDTH)

    def scores(step):
        g, layer, pair = step
        source = (first_ref, second_ref)[layer]
        head = g * group + pair * PAIR
        query = jnp.concatenate(
            [source[:, (head + i) * HEAD_WIDTH : (head + i + 1) * HEAD_WIDTH] for i in range(PAIR)], axis=0
        )
        keys = jnp.concatenate([b[g] for b in blocks], axis=0)
        return lax.dot_general(keys, query, (((1,), (1,)), ((), ())), preferred_element_type=jnp.float32)

    def absorb():
        place = query_base + lax.broadcasted_iota(jnp.int32, (1, tokens), 1)
        start = start_of(place)
        for i, base in enumerate(bases):
            key_place = base + lax.broadcasted_iota(jnp.int32, (tokens, tokens), 0)
            visible = (key_place >= start) & (key_place <= place)
            bias = jnp.where(visible, 0.0, HIDDEN)
            for j in range(PAIR):
                bias_ref[i * tokens : (i + 1) * tokens, j * tokens : (j + 1) * tokens] = bias

        ahead = scores(steps[0])
        for n, step in enumerate(steps):
            g, _, _ = step
            raw = ahead
            if n + 1 < len(steps):
                ahead = scores(steps[n + 1])
            masked = raw * factor + bias_ref[...]
            highest = jnp.max(masked, axis=0, keepdims=True)
            if not first:
                former = stat_in[2 * n : 2 * n + 1, :]
                highest = jnp.maximum(highest, former)
            weights = jnp.exp2(masked - highest)
            row_sum = jnp.sum(weights, axis=0, keepdims=True)
            values = jnp.concatenate([b[KEY_VALUE_HEADS + g] for b in blocks], axis=1)
            product = jnp.dot(values, weights.astype(jnp.bfloat16), preferred_element_type=jnp.float32)
            if not first:
                fade = jnp.exp2(former - highest)
                row_sum = row_sum + stat_in[2 * n + 1 : 2 * n + 2, :] * fade
                product = product + sum_in[n] * fade
            finish(n, step, product, row_sum, highest)

    def finish(n, step, product, row_sum, highest):
        g, layer, pair = step
        if last:
            blended = product * (1.0 / row_sum)
            head = g * group + pair * PAIR
            for i in range(PAIR):
                columns = slice((head + i) * HEAD_WIDTH, (head + i + 1) * HEAD_WIDTH)
                out_refs[layer][:, columns] = blended[:, i * tokens : (i + 1) * tokens].T.astype(jnp.bfloat16)
        else:
            sum_ref[n] = product
            stat_ref[2 * n : 2 * n + 1, :] = highest
            stat_ref[2 * n + 1 : 2 * n + 2, :] = row_sum

    if first:
        absorb()
    else:
        pl.when(needed)(absorb)

        @pl.when(jnp.logical_not(needed))
        def _():
            for n, step in enumerate(steps):
                finish(n, step, sum_in[n], stat_in[2 * n + 1 : 2 * n + 2, :], stat_in[2 * n : 2 * n + 1, :])


def attend(device, lengths, first_queries, second_queries, blocks, sources, state, last):
    tokens = first_queries.shape[0]
    steps = 2 * QUERY_HEAD_COUNT // PAIR
    width = PAIR * tokens
    state_shapes = [
        jax.ShapeDtypeStruct((steps, HEAD_WIDTH, width), jnp.float32),
        jax.ShapeDtypeStruct((2 * steps, width), jnp.float32),
    ]
    in_vmem = pl.BlockSpec(memory_space=pltpu.VMEM)
    in_smem = pl.BlockSpec(memory_space=pltpu.SMEM)
    first = state is None
    operands = [device, lengths, first_queries, second_queries, *blocks]
    aliases = {}
    if not first:
        if not last:
            aliases = {len(operands): 0, len(operands) + 1: 1}
        operands += state
    keys = len(blocks) * tokens
    outs = state_shapes
    if last:
        outs = [jax.ShapeDtypeStruct(q.shape, q.dtype) for q in (first_queries, second_queries)]
    return pl.pallas_call(
        functools.partial(attend_kernel, sources, len(blocks), first, last),
        out_shape=outs,
        in_specs=[in_smem, in_smem] + [in_vmem] * (len(operands) - 2),
        out_specs=[in_vmem] * 2,
        scratch_shapes=[pltpu.VMEM((keys, width), jnp.float32)],
        input_output_aliases=aliases,
        cost_estimate=pl.CostEstimate(
            flops=steps * 4 * keys * width * HEAD_WIDTH,
            bytes_accessed=2 * first_queries.size * 2 + 2 * keys * 2 * KEY_VALUE_HEADS * HEAD_WIDTH,
            transcendentals=steps * keys * width,
        ),
        compiler_params=pltpu.CompilerParams(vmem_limit_bytes=16 * 1024 * 1024),
        name="attend_last" if last else "attend",
    )(*operands)


def on_device(first_queries, second_queries, common_keys, common_values, lengths):
    members = lax.axis_size("seq")
    rounds = members // 2 // LEVEL
    device = lax.axis_index("seq").astype(jnp.int32).reshape(1)

    def send(block, route):
        return lax.ppermute(block, "seq", route)

    def core(block):
        return send(block, swapped(members, CORE))

    def row(block):
        return send(block, swapped(members, ROW))

    def behind(levels, flip):
        return lambda d: (d ^ flip) - levels * LEVEL

    def upper_behind(levels, flip):
        return lambda d: jnp.where(d & ROW == 0, (d ^ flip) - levels * LEVEL, NOWHERE)

    own = pack(common_keys, common_values)
    step = functools.partial(attend, device, lengths, first_queries, second_queries)

    previous = send(own, shifted(members))
    beside = row(own)
    partner = core(own)
    state = step([own, partner], [behind(0, 0), behind(0, CORE)], None, False)

    blocks, sources = [beside, core(beside)], [behind(0, ROW), behind(0, ROW | CORE)]
    for level in range(1, rounds):
        blocks += [previous, core(previous)]
        sources += [behind(level, 0), behind(level, CORE)]
        following = send(previous, shifted(members))
        over = row(previous)
        if level == rounds - 1:
            corner = send(previous, across(members))
        state = step(blocks, sources, state, False)
        blocks, sources = [over, core(over)], [behind(level, ROW), behind(level, ROW | CORE)]
        previous = following
    blocks += [previous, core(previous)]
    sources += [behind(rounds, 0), behind(rounds, CORE)]
    state = step(blocks, sources, state, False)
    return tuple(
        step(
            [corner, core(corner)],
            [upper_behind(rounds, ROW), upper_behind(rounds, ROW | CORE)],
            state,
            True,
        )
    )


def solution(mesh):
    tokens = P(("groups", "seq"), None)
    return jax.shard_map(
        on_device,
        mesh=mesh,
        in_specs=(tokens, tokens, tokens, tokens, P("groups")),
        out_specs=(tokens, tokens),
        check_vma=False,
    )
```

time: 142 us -> 50.5 us (0.36)
  the two profiles are of different devices: /device:TPU:0 before, /device:TPU:17 now
where the time goes in v1:
time: 50.5 us; the launch traced here: 50.2 us
  Pallas kernels  19.1 us (38%)
  starting transfers between devices  19.1 us (38%)
  waiting for transfers between devices  7.56 us (15%)
  local copies, waits for them, and re-layouts  3.69 us (7%)
  between operations  0.75 us (1%)
    ppermute x11, starting transfers between devices, send(): return lax.ppermute(block, 'seq', route)  19.1 us
    pallas_call x4, Pallas kernels, attend(): pl.pallas_call(functools.partial(attend_kernel, sources, len(blocks), fir...  17.3 us
    ppermute x11, waiting for transfers between devices, send(): return lax.ppermute(block, 'seq', route)  7.56 us
    unnamed x10, local copies, waits for them, and re-layouts  3.69 us
    pallas_call x1, Pallas kernels, pack(): pl.pallas_call(pack_kernel, out_shape=jax.ShapeDtypeStruct((2 * KEY_VALUE...  1.82 us
  transfers between devices with their start and end apart: 11, of which 2 were waited for; matrix products, arithmetic and copies ran while one was open for 0% of the time, Pallas kernels for 26%

profile of v1, /device:TPU:17, one launch (start us, length us, event | category | flops | bytes accessed | tf_op | source)
XLA Modules:
  0.0 50.2 jit_solution(17689409618348276632)
XLA Ops:
  0.6 0.0 copy-start.1
  0.6 1.8 %pack.1.refs_4_ = bf16[8,128,128]{2,1,0:T(8,128)(2,1)} custom-call(bf16[128,512]{1,0:T(8,128)(2,1)} %keys_ref.1, bf16[128,512]{1,0:T(8,128)(2,1)} %values_ref.1), custom_call_target="tpu_custom_call" | custom-call | tf_op jit(solution)/shard_map/pack/pallas_call | solution.py:46
  2.5 3.2 %collective-permute-start = (bf16[8,128,128]{2,1,0:T(8,128)(2,1)}, bf16[8,128,128]{2,1,0:T(8,128)(2,1)S(1)}, u32[]{:S(2)}, u32[]{:S(2)}) collective-permute-start(bf16[8,128,128]{2,1,0:T(8,128)(2,1)} %pack.1.refs_4_), channel_id=1, source_target_pairs={{0,4},{1,5},{2,6},{3,7},{4,8},{5,9},{6,10},{7,11},{8,12},{9,13},{1... | collective-permute-start | bytes 786440 | tf_op jit(solution)/shard_map/ppermute | solution.py:208
  5.7 1.0 %collective-permute-start.10 = (bf16[8,128,128]{2,1,0:T(8,128)(2,1)}, bf16[8,128,128]{2,1,0:T(8,128)(2,1)S(1)}, u32[]{:S(2)}, u32[]{:S(2)}) collective-permute-start(bf16[8,128,128]{2,1,0:T(8,128)(2,1)} %pack.1.refs_4_), channel_id=1, source_target_pairs={{0,1},{1,0},{2,3},{3,2},{4,5},{5,4},{6,7},{7,6},{8,9},{9,8},{10,11... | collective-permute-start | bytes 786440 | tf_op jit(solution)/shard_map/ppermute | solution.py:208
  6.7 1.2 %collective-permute-start.7 = (bf16[8,128,128]{2,1,0:T(8,128)(2,1)}, bf16[8,128,128]{2,1,0:T(8,128)(2,1)S(1)}, u32[]{:S(2)}, u32[]{:S(2)}) collective-permute-start(bf16[8,128,128]{2,1,0:T(8,128)(2,1)} %pack.1.refs_4_), channel_id=1, source_target_pairs={{0,2},{1,3},{2,0},{3,1},{4,6},{5,7},{6,4},{7,5},{8,10},{9,11},{10,... | collective-permute-start | bytes 786440 | tf_op jit(solution)/shard_map/ppermute | solution.py:208
  7.9 3.8 %collective-permute-done.refs_6_ = bf16[8,128,128]{2,1,0:T(8,128)(2,1)S(1)} collective-permute-done((bf16[8,128,128]{2,1,0:T(8,128)(2,1)}, bf16[8,128,128]{2,1,0:T(8,128)(2,1)S(1)}, u32[]{:S(2)}, u32[]{:S(2)}) %collective-permute-start) | collective-permute-done | bytes 262176 | tf_op jit(solution)/shard_map/ppermute | solution.py:208
  11.7 1.2 %collective-permute-start.3 = (bf16[8,128,128]{2,1,0:T(8,128)(2,1)S(1)}, bf16[8,128,128]{2,1,0:T(8,128)(2,1)S(1)}, u32[]{:S(2)}, u32[]{:S(2)}) collective-permute-start(bf16[8,128,128]{2,1,0:T(8,128)(2,1)S(1)} %collective-permute-done.refs_6_), channel_id=1, source_target_pairs={{0,2},{1,3},{2,0},{3,1},{4,6},{5,7},{6,4},{7,5},{8,10},{9,11},{10,... | collective-permute-start | bytes 786440 | tf_op jit(solution)/shard_map/ppermute | solution.py:208
  13.0 3.2 %collective-permute-start.5 = (bf16[8,128,128]{2,1,0:T(8,128)(2,1)S(1)}, bf16[8,128,128]{2,1,0:T(8,128)(2,1)S(1)}, u32[]{:S(2)}, u32[]{:S(2)}) collective-permute-start(bf16[8,128,128]{2,1,0:T(8,128)(2,1)S(1)} %collective-permute-done.refs_6_), channel_id=1, source_target_pairs={{0,4},{1,5},{2,6},{3,7},{4,8},{5,9},{6,10},{7,11},{8,12},{9,13},{1... | collective-permute-start | bytes 786440 | tf_op jit(solution)/shard_map/ppermute | solution.py:208
  16.2 1.3 %collective-permute-start.1 = (bf16[8,128,128]{2,1,0:T(8,128)(2,1)S(1)}, bf16[8,128,128]{2,1,0:T(8,128)(2,1)S(1)}, u32[]{:S(2)}, u32[]{:S(2)}) collective-permute-start(bf16[8,128,128]{2,1,0:T(8,128)(2,1)S(1)} %collective-permute-done.refs_6_), channel_id=1, source_target_pairs={{2,4},{3,5},{6,8},{7,9},{10,12},{11,13},{18,20},{19,21},{22,24},{2... | collective-permute-start | bytes 786440 | tf_op jit(solution)/shard_map/ppermute | solution.py:208
  17.5 0.0 collective-permute-done.10.refs_5_
  17.5 2.2 %collective-permute-start.9 = (bf16[8,128,128]{2,1,0:T(8,128)(2,1)S(1)}, bf16[8,128,128]{2,1,0:T(8,128)(2,1)S(1)}, u32[]{:S(2)}, u32[]{:S(2)}) collective-permute-start(bf16[8,128,128]{2,1,0:T(8,128)(2,1)S(1)} %collective-permute-done.refs_6_), channel_id=1, source_target_pairs={{0,1},{1,0},{2,3},{3,2},{4,5},{5,4},{6,7},{7,6},{8,9},{9,8},{10,11... | collective-permute-start | bytes 786440 | tf_op jit(solution)/shard_map/ppermute | solution.py:208
  19.6 0.0 collective-permute-done.7.refs_4_
  19.7 0.1 collective-permute-start.8
  19.7 0.0 collective-permute-done.3.refs_4_
  19.7 1.5 %collective-permute-start.4 = (bf16[8,128,128]{2,1,0:T(8,128)(2,1)S(1)}, bf16[8,128,128]{2,1,0:T(8,128)(2,1)S(1)}, u32[]{:S(2)}, u32[]{:S(2)}) collective-permute-start(bf16[8,128,128]{2,1,0:T(8,128)(2,1)S(1)} %collective-permute-done.3.refs_4_), channel_id=1, source_target_pairs={{0,1},{1,0},{2,3},{3,2},{4,5},{5,4},{6,7},{7,6},{8,9},{9,8},{10,11... | collective-permute-start | bytes 786440 | tf_op jit(solution)/shard_map/ppermute | solution.py:208
  21.2 0.0 collective-permute-done.5.refs_6_
  21.2 2.4 %collective-permute-start.6 = (bf16[8,128,128]{2,1,0:T(8,128)(2,1)S(1)}, bf16[8,128,128]{2,1,0:T(8,128)(2,1)S(1)}, u32[]{:S(2)}, u32[]{:S(2)}) collective-permute-start(bf16[8,128,128]{2,1,0:T(8,128)(2,1)S(1)} %collective-permute-done.5.refs_6_), channel_id=1, source_target_pairs={{0,1},{1,0},{2,3},{3,2},{4,5},{5,4},{6,7},{7,6},{8,9},{9,8},{10,11... | collective-permute-start | bytes 786440 | tf_op jit(solution)/shard_map/ppermute | solution.py:208
  23.6 3.7 %collective-permute-done.1.refs_4_ = bf16[8,128,128]{2,1,0:T(8,128)(2,1)S(1)} collective-permute-done((bf16[8,128,128]{2,1,0:T(8,128)(2,1)S(1)}, bf16[8,128,128]{2,1,0:T(8,128)(2,1)S(1)}, u32[]{:S(2)}, u32[]{:S(2)}) %collective-permute-start.1) | collective-permute-done | bytes 262176 | tf_op jit(solution)/shard_map/ppermute | solution.py:208
  27.3 1.8 %collective-permute-start.2 = (bf16[8,128,128]{2,1,0:T(8,128)(2,1)S(1)}, bf16[8,128,128]{2,1,0:T(8,128)(2,1)S(1)}, u32[]{:S(2)}, u32[]{:S(2)}) collective-permute-start(bf16[8,128,128]{2,1,0:T(8,128)(2,1)S(1)} %collective-permute-done.1.refs_4_), channel_id=1, source_target_pairs={{0,1},{1,0},{2,3},{3,2},{4,5},{5,4},{6,7},{7,6},{8,9},{9,8},{10,11... | collective-permute-start | bytes 786440 | tf_op jit(solution)/shard_map/ppermute | solution.py:208
  29.1 1.0 %copy-done = bf16[128,2048]{1,0:T(8,128)(2,1)S(1)} copy-done((bf16[128,2048]{1,0:T(8,128)(2,1)S(1)}, bf16[128,2048]{1,0:T(8,128)(2,1)}, u32[]{:S(2)}) %copy-start) | copy-done | bytes 524312
  30.2 1.0 %copy-done.2 = bf16[128,2048]{1,0:T(8,128)(2,1)S(1)} copy-done((bf16[128,2048]{1,0:T(8,128)(2,1)S(1)}, bf16[128,2048]{1,0:T(8,128)(2,1)}, u32[]{:S(2)}) %copy-start.2) | copy-done | bytes 524312
  31.2 0.9 %copy-done.3 = bf16[8,128,128]{2,1,0:T(8,128)(2,1)S(1)} copy-done((bf16[8,128,128]{2,1,0:T(8,128)(2,1)S(1)}, bf16[8,128,128]{2,1,0:T(8,128)(2,1)}, u32[]{:S(2)}) %copy-start.3) | copy-done | bytes 262168
  32.2 0.7 %copy-done.4 = s32[4]{0:T(128)S(1)} copy-done((s32[4]{0:T(128)S(1)}, s32[4]{0:T(128)}, u32[]{:S(2)}) %copy-start.4) | copy-done | bytes 40
  32.8 3.1 %attend.3 = (f32[16,128,256]{2,1,0:T(8,128)S(1)}, f32[32,256]{1,0:T(8,128)S(1)}) custom-call(s32[1]{0:T(128)} %bitcast.refs_0_, s32[4]{0:T(128)S(1)} %copy-done.4, bf16[128,2048]{1,0:T(8,128)(2,1)S(1)} %copy-done, bf16[128,2048]{1,0:T(8,128)(2,1)S(1)} %copy-done.2, bf16[8,128,128]{2,1,0:T(8,128)(2,1)S(1)} %copy-done.3, ...), custom_call_target="tpu_custom_call" | custom-call | flops 536870912 | bytes 1572864 | tf_op jit(solution)/shard_map/attend/pallas_call | solution.py:185
  35.9 0.0 collective-permute-done.9.refs_7_
  35.9 0.0 collective-permute-done.8.refs_5_
  36.0 4.9 %attend.4 = (f32[16,128,256]{2,1,0:T(8,128)S(1)}, f32[32,256]{1,0:T(8,128)S(1)}) custom-call(s32[1]{0:T(128)} %bitcast.refs_0_, s32[4]{0:T(128)S(1)} %copy-done.4, bf16[128,2048]{1,0:T(8,128)(2,1)S(1)} %copy-done.1, bf16[128,2048]{1,0:T(8,128)(2,1)S(1)} %copy-done.2, ...), custom_call_target="tpu_custom_call", output_to_operand_aliasing={{0}: (8, {}), {1}: (9, {})} | custom-call | flops 1073741824 | bytes 2097152 | tf_op jit(solution)/shard_map/attend/pallas_call | solution.py:185
  40.8 0.0 collective-permute-done.4.refs_5_
  40.8 0.0 collective-permute-done.6.refs_7_
  40.8 5.1 %attend.5 = (f32[16,128,256]{2,1,0:T(8,128)S(1)}, f32[32,256]{1,0:T(8,128)S(1)}) custom-call(s32[1]{0:T(128)} %bitcast.refs_0_, s32[4]{0:T(128)S(1)} %copy-done.4, bf16[128,2048]{1,0:T(8,128)(2,1)S(1)} %copy-done.1, bf16[128,2048]{1,0:T(8,128)(2,1)S(1)} %copy-done.2, ...), custom_call_target="tpu_custom_call", output_to_operand_aliasing={{0}: (8, {}), {1}: (9, {})} | custom-call | flops 1073741824 | bytes 2097152 | tf_op jit(solution)/shard_map/attend/pallas_call | solution.py:185
  45.9 0.0 collective-permute-done.2.refs_5_
  45.9 4.3 %attend_last.1 = (bf16[128,2048]{1,0:T(8,128)(2,1)}, bf16[128,2048]{1,0:T(8,128)(2,1)}) custom-call(s32[1]{0:T(128)} %bitcast.refs_0_, s32[4]{0:T(128)S(1)} %copy-done.4, bf16[128,2048]{1,0:T(8,128)(2,1)S(1)} %copy-done.1, bf16[128,2048]{1,0:T(8,128)(2,1)S(1)} %copy-done.2, bf16[8,128,128]{2,1,0:T(8,128)(2,1)S(1)} %collective-permute-done.1.refs_4_, ...), custom_call_target="tpu_custom_call" | custom-call | flops 536870912 | bytes 1572864 | tf_op jit(solution)/shard_map/attend_last/pallas_call | solution.py:185
  (5 shorter events, 0.0 us)
Async XLA Ops:
  0.6 35.3 %copy-start.1 = (bf16[128,2048]{1,0:T(8,128)(2,1)S(1)}, bf16[128,2048]{1,0:T(8,128)(2,1)}, u32[]{:S(2)}) copy-start(bf16[128,2048]{1,0:T(8,128)(2,1)} %refs_2_.7) | copy-start | bytes 1572868
  2.5 9.3 %collective-permute-start = (bf16[8,128,128]{2,1,0:T(8,128)(2,1)}, bf16[8,128,128]{2,1,0:T(8,128)(2,1)S(1)}, u32[]{:S(2)}, u32[]{:S(2)}) collective-permute-start(bf16[8,128,128]{2,1,0:T(8,128)(2,1)} %pack.1.refs_4_), channel_id=1, source_target_pairs={{0,4},{1,5},{2,6},{3,7},{4,8},{5,9},{6,10},{7,11},{8,12},{9,13},{1... | collective-permute-start | bytes 786440 | tf_op jit(solution)/shard_map/ppermute | solution.py:208
  5.7 11.8 %collective-permute-start.10 = (bf16[8,128,128]{2,1,0:T(8,128)(2,1)}, bf16[8,128,128]{2,1,0:T(8,128)(2,1)S(1)}, u32[]{:S(2)}, u32[]{:S(2)}) collective-permute-start(bf16[8,128,128]{2,1,0:T(8,128)(2,1)} %pack.1.refs_4_), channel_id=1, source_target_pairs={{0,1},{1,0},{2,3},{3,2},{4,5},{5,4},{6,7},{7,6},{8,9},{9,8},{10,11... | collective-permute-start | bytes 786440 | tf_op jit(solution)/shard_map/ppermute | solution.py:208
  6.7 13.0 %collective-permute-start.7 = (bf16[8,128,128]{2,1,0:T(8,128)(2,1)}, bf16[8,128,128]{2,1,0:T(8,128)(2,1)S(1)}, u32[]{:S(2)}, u32[]{:S(2)}) collective-permute-start(bf16[8,128,128]{2,1,0:T(8,128)(2,1)} %pack.1.refs_4_), channel_id=1, source_target_pairs={{0,2},{1,3},{2,0},{3,1},{4,6},{5,7},{6,4},{7,5},{8,10},{9,11},{10,... | collective-permute-start | bytes 786440 | tf_op jit(solution)/shard_map/ppermute | solution.py:208
  11.7 8.0 %collective-permute-start.3 = (bf16[8,128,128]{2,1,0:T(8,128)(2,1)S(1)}, bf16[8,128,128]{2,1,0:T(8,128)(2,1)S(1)}, u32[]{:S(2)}, u32[]{:S(2)}) collective-permute-start(bf16[8,128,128]{2,1,0:T(8,128)(2,1)S(1)} %collective-permute-done.refs_6_), channel_id=1, source_target_pairs={{0,2},{1,3},{2,0},{3,1},{4,6},{5,7},{6,4},{7,5},{8,10},{9,11},{10,... | collective-permute-start | bytes 786440 | tf_op jit(solution)/shard_map/ppermute | solution.py:208
  13.0 8.3 %collective-permute-start.5 = (bf16[8,128,128]{2,1,0:T(8,128)(2,1)S(1)}, bf16[8,128,128]{2,1,0:T(8,128)(2,1)S(1)}, u32[]{:S(2)}, u32[]{:S(2)}) collective-permute-start(bf16[8,128,128]{2,1,0:T(8,128)(2,1)S(1)} %collective-permute-done.refs_6_), channel_id=1, source_target_pairs={{0,4},{1,5},{2,6},{3,7},{4,8},{5,9},{6,10},{7,11},{8,12},{9,13},{1... | collective-permute-start | bytes 786440 | tf_op jit(solution)/shard_map/ppermute | solution.py:208
  16.2 11.1 %collective-permute-start.1 = (bf16[8,128,128]{2,1,0:T(8,128)(2,1)S(1)}, bf16[8,128,128]{2,1,0:T(8,128)(2,1)S(1)}, u32[]{:S(2)}, u32[]{:S(2)}) collective-permute-start(bf16[8,128,128]{2,1,0:T(8,128)(2,1)S(1)} %collective-permute-done.refs_6_), channel_id=1, source_target_pairs={{2,4},{3,5},{6,8},{7,9},{10,12},{11,13},{18,20},{19,21},{22,24},{2... | collective-permute-start | bytes 786440 | tf_op jit(solution)/shard_map/ppermute | solution.py:208
  17.5 18.4 %collective-permute-start.9 = (bf16[8,128,128]{2,1,0:T(8,128)(2,1)S(1)}, bf16[8,128,128]{2,1,0:T(8,128)(2,1)S(1)}, u32[]{:S(2)}, u32[]{:S(2)}) collective-permute-start(bf16[8,128,128]{2,1,0:T(8,128)(2,1)S(1)} %collective-permute-done.refs_6_), channel_id=1, source_target_pairs={{0,1},{1,0},{2,3},{3,2},{4,5},{5,4},{6,7},{7,6},{8,9},{9,8},{10,11... | collective-permute-start | bytes 786440 | tf_op jit(solution)/shard_map/ppermute | solution.py:208
  19.7 16.3 %collective-permute-start.8 = (bf16[8,128,128]{2,1,0:T(8,128)(2,1)S(1)}, bf16[8,128,128]{2,1,0:T(8,128)(2,1)S(1)}, u32[]{:S(2)}, u32[]{:S(2)}) collective-permute-start(bf16[8,128,128]{2,1,0:T(8,128)(2,1)S(1)} %collective-permute-done.7.refs_4_), channel_id=1, source_target_pairs={{0,1},{1,0},{2,3},{3,2},{4,5},{5,4},{6,7},{7,6},{8,9},{9,8},{10,11... | collective-permute-start | bytes 786440 | tf_op jit(solution)/shard_map/ppermute | solution.py:208
  19.7 21.1 %collective-permute-start.4 = (bf16[8,128,128]{2,1,0:T(8,128)(2,1)S(1)}, bf16[8,128,128]{2,1,0:T(8,128)(2,1)S(1)}, u32[]{:S(2)}, u32[]{:S(2)}) collective-permute-start(bf16[8,128,128]{2,1,0:T(8,128)(2,1)S(1)} %collective-permute-done.3.refs_4_), channel_id=1, source_target_pairs={{0,1},{1,0},{2,3},{3,2},{4,5},{5,4},{6,7},{7,6},{8,9},{9,8},{10,11... | collective-permute-start | bytes 786440 | tf_op jit(solution)/shard_map/ppermute | solution.py:208
  21.2 19.6 %collective-permute-start.6 = (bf16[8,128,128]{2,1,0:T(8,128)(2,1)S(1)}, bf16[8,128,128]{2,1,0:T(8,128)(2,1)S(1)}, u32[]{:S(2)}, u32[]{:S(2)}) collective-permute-start(bf16[8,128,128]{2,1,0:T(8,128)(2,1)S(1)} %collective-permute-done.5.refs_6_), channel_id=1, source_target_pairs={{0,1},{1,0},{2,3},{3,2},{4,5},{5,4},{6,7},{7,6},{8,9},{9,8},{10,11... | collective-permute-start | bytes 786440 | tf_op jit(solution)/shard_map/ppermute | solution.py:208
  27.3 18.6 %collective-permute-start.2 = (bf16[8,128,128]{2,1,0:T(8,128)(2,1)S(1)}, bf16[8,128,128]{2,1,0:T(8,128)(2,1)S(1)}, u32[]{:S(2)}, u32[]{:S(2)}) collective-permute-start(bf16[8,128,128]{2,1,0:T(8,128)(2,1)S(1)} %collective-permute-done.1.refs_4_), channel_id=1, source_target_pairs={{0,1},{1,0},{2,3},{3,2},{4,5},{5,4},{6,7},{7,6},{8,9},{9,8},{10,11... | collective-permute-start | bytes 786440 | tf_op jit(solution)/shard_map/ppermute | solution.py:208
  29.1 1.0 %copy-start = (bf16[128,2048]{1,0:T(8,128)(2,1)S(1)}, bf16[128,2048]{1,0:T(8,128)(2,1)}, u32[]{:S(2)}) copy-start(bf16[128,2048]{1,0:T(8,128)(2,1)} %refs_2_.7) | copy-start | bytes 1572868
  30.2 1.0 %copy-start.2 = (bf16[128,2048]{1,0:T(8,128)(2,1)S(1)}, bf16[128,2048]{1,0:T(8,128)(2,1)}, u32[]{:S(2)}) copy-start(bf16[128,2048]{1,0:T(8,128)(2,1)} %refs_3_.7) | copy-start | bytes 1572868
  31.2 0.9 %copy-start.3 = (bf16[8,128,128]{2,1,0:T(8,128)(2,1)S(1)}, bf16[8,128,128]{2,1,0:T(8,128)(2,1)}, u32[]{:S(2)}) copy-start(bf16[8,128,128]{2,1,0:T(8,128)(2,1)} %pack.1.refs_4_) | copy-start | bytes 786436
  32.2 0.7 %copy-start.4 = (s32[4]{0:T(128)S(1)}, s32[4]{0:T(128)}, u32[]{:S(2)}) copy-start(s32[4]{0:T(128)} %refs_1_.7) | copy-start | bytes 52

commit v2 on v1

--- a/solution.py
+++ b/solution.py
@@ -20,6 +20,11 @@
 HIDDEN = -1e30
 NOWHERE = -(1 << 20)
 PAIR = 2
+AHEAD = 2
+BEHIND = 1
+
+GRANT = 16 << 20
+SMALL_GRANT = 4 << 20
 
 
 def swapped(count, distance):
@@ -34,11 +39,19 @@
     return [(d, d + LEVEL - ROW) for d in range(count - LEVEL) if d & ROW]
 
 
-def pack_kernel(keys_ref, values_ref, packed_ref):
+def pack_kernel(keys_ref, values_ref, packed_ref, keys_here, values_here, arrived):
+    copies = [
+        pltpu.make_async_copy(keys_ref, keys_here, arrived.at[0]),
+        pltpu.make_async_copy(values_ref, values_here, arrived.at[1]),
+    ]
+    for copy in copies:
+        copy.start()
+    copies[0].wait()
     for g in range(KEY_VALUE_HEADS):
-        columns = pl.ds(g * HEAD_WIDTH, HEAD_WIDTH)
-        packed_ref[g] = keys_ref[:, columns]
-        packed_ref[KEY_VALUE_HEADS + g] = values_ref[:, columns].T
+        packed_ref[g] = keys_here[:, g * HEAD_WIDTH : (g + 1) * HEAD_WIDTH]
+    copies[1].wait()
+    for g in range(KEY_VALUE_HEADS):
+        packed_ref[KEY_VALUE_HEADS + g] = values_here[:, g * HEAD_WIDTH : (g + 1) * HEAD_WIDTH].T
 
 
 def pack(keys, values):
@@ -46,8 +59,16 @@
     return pl.pallas_call(
         pack_kernel,
         out_shape=jax.ShapeDtypeStruct((2 * KEY_VALUE_HEADS, tokens, HEAD_WIDTH), keys.dtype),
+        in_specs=[pl.BlockSpec(memory_space=pltpu.HBM)] * 2,
+        out_specs=pl.BlockSpec(memory_space=pltpu.VMEM),
+        scratch_shapes=[
+            pltpu.VMEM(keys.shape, keys.dtype),
+            pltpu.VMEM(values.shape, values.dtype),
+            pltpu.SemaphoreType.DMA((2,)),
+        ],
+        compiler_params=pltpu.CompilerParams(vmem_limit_bytes=SMALL_GRANT),
         name="pack",
-    )(keys, values)
+    )(*[pltpu.with_memory_space_constraint(a, pltpu.HBM) for a in (keys, values)])
 
 
 def attend_kernel(sources, count, first, last, *refs):
@@ -59,7 +80,8 @@
         sum_in, stat_in = rest[:2]
         rest = rest[2:]
     if last:
-        out_refs, rest = rest[:2], rest[2:]
+        gone_refs, rest = rest[:2], rest[2:]
+        out_refs, left, rest = rest[:2], rest[2], rest[3:]
     else:
         sum_ref, stat_ref = rest[:2]
         rest = rest[2:]
@@ -82,83 +104,110 @@
             start = jnp.where(place >= bound, bound, start)
         return start
 
-    bases = []
-    for source in sources:
-        bases.append(source(device) * tokens)
+    bases = [source(device) * tokens for source in sources]
     earliest = start_of(query_base)
-    needed = functools.reduce(
-        jnp.logical_or,
-        [(b <= query_base + tokens - 1) & (b + tokens - 1 >= earliest) for b in bases],
-    )
+
+    def needed(i):
+        return (bases[i] <= query_base + tokens - 1) & (bases[i] + tokens - 1 >= earliest)
 
     group = QUERY_HEAD_COUNT // KEY_VALUE_HEADS
     pairs = group // PAIR
     steps = [(g, layer, pair) for g in range(KEY_VALUE_HEADS) for layer in range(2) for pair in range(pairs)]
     factor = math.log2(math.e) / math.sqrt(HEAD_WIDTH)
 
-    def scores(step):
+    def scores(step, active):
         g, layer, pair = step
         source = (first_ref, second_ref)[layer]
         head = g * group + pair * PAIR
         query = jnp.concatenate(
             [source[:, (head + i) * HEAD_WIDTH : (head + i + 1) * HEAD_WIDTH] for i in range(PAIR)], axis=0
         )
-        keys = jnp.concatenate([b[g] for b in blocks], axis=0)
+        keys = jnp.concatenate([blocks[i][g] for i in active], axis=0)
         return lax.dot_general(keys, query, (((1,), (1,)), ((), ())), preferred_element_type=jnp.float32)
 
-    def absorb():
+    def weigh(n, raw):
+        masked = raw * factor + bias_ref[: raw.shape[0], :]
+        highest = jnp.max(masked, axis=0, keepdims=True)
+        fade = None
+        if not first:
+            former = stat_in[2 * n : 2 * n + 1, :]
+            highest = jnp.maximum(highest, former)
+            fade = jnp.exp2(former - highest)
+        weights = jnp.exp2(masked - highest)
+        row_sum = jnp.sum(weights, axis=0, keepdims=True)
+        return n, weights.astype(jnp.bfloat16), highest, fade, row_sum
+
+    def gather(active, n, rounded, highest, fade, row_sum):
+        values = jnp.concatenate([blocks[i][KEY_VALUE_HEADS + steps[n][0]] for i in active], axis=1)
+        product = jnp.dot(values, rounded, preferred_element_type=jnp.float32)
+        if not first:
+            row_sum = row_sum + stat_in[2 * n + 1 : 2 * n + 2, :] * fade
+            product = product + sum_in[n] * fade
+        finish(n, steps[n], product, row_sum, highest)
+
+    def absorb(active):
         place = query_base + lax.broadcasted_iota(jnp.int32, (1, tokens), 1)
         start = start_of(place)
-        for i, base in enumerate(bases):
-            key_place = base + lax.broadcasted_iota(jnp.int32, (tokens, tokens), 0)
+        for row, i in enumerate(active):
+            key_place = bases[i] + lax.broadcasted_iota(jnp.int32, (tokens, tokens), 0)
             visible = (key_place >= start) & (key_place <= place)
             bias = jnp.where(visible, 0.0, HIDDEN)
             for j in range(PAIR):
-                bias_ref[i * tokens : (i + 1) * tokens, j * tokens : (j + 1) * tokens] = bias
-
-        ahead = scores(steps[0])
-        for n, step in enumerate(steps):
-            g, _, _ = step
-            raw = ahead
-            if n + 1 < len(steps):
-                ahead = scores(steps[n + 1])
-            masked = raw * factor + bias_ref[...]
-            highest = jnp.max(masked, axis=0, keepdims=True)
-            if not first:
-                former = stat_in[2 * n : 2 * n + 1, :]
-                highest = jnp.maximum(highest, former)
-            weights = jnp.exp2(masked - highest)
-            row_sum = jnp.sum(weights, axis=0, keepdims=True)
-            values = jnp.concatenate([b[KEY_VALUE_HEADS + g] for b in blocks], axis=1)
-            product = jnp.dot(values, weights.astype(jnp.bfloat16), preferred_element_type=jnp.float32)
-            if not first:
-                fade = jnp.exp2(former - highest)
-                row_sum = row_sum + stat_in[2 * n + 1 : 2 * n + 2, :] * fade
-                product = product + sum_in[n] * fade
-            finish(n, step, product, row_sum, highest)
+                bias_ref[row * tokens : (row + 1) * tokens, j * tokens : (j + 1) * tokens] = bias
+
+        early = [scores(step, active) for step in steps[:AHEAD]]
+        late = []
+        for n in range(len(steps)):
+            if n + AHEAD < len(steps):
+                early.append(scores(steps[n + AHEAD], active))
+            if len(late) > BEHIND:
+                gather(active, *late.pop(0))
+            late.append(weigh(n, early.pop(0)))
+        for item in late:
+            gather(active, *item)
+
+    def leaving(n):
+        g, layer, pair = steps[n]
+        columns = pl.ds((g * group + pair * PAIR) * HEAD_WIDTH, PAIR * HEAD_WIDTH)
+        return pltpu.make_async_copy(out_refs[layer].at[:, columns], gone_refs[layer].at[:, columns], left.at[n])
 
     def finish(n, step, product, row_sum, highest):
         g, layer, pair = step
         if last:
-            blended = product * (1.0 / row_sum)
+            blended = (product * (1.0 / row_sum)).astype(jnp.bfloat16)
             head = g * group + pair * PAIR
             for i in range(PAIR):
                 columns = slice((head + i) * HEAD_WIDTH, (head + i + 1) * HEAD_WIDTH)
-                out_refs[layer][:, columns] = blended[:, i * tokens : (i + 1) * tokens].T.astype(jnp.bfloat16)
+                out_refs[layer][:, columns] = blended[:, i * tokens : (i + 1) * tokens].T
+            leaving(n).start()
         else:
             sum_ref[n] = product
             stat_ref[2 * n : 2 * n + 1, :] = highest
             stat_ref[2 * n + 1 : 2 * n + 2, :] = row_sum
 
     if first:
-        absorb()
+        both = needed(1)
+        pl.when(both)(lambda: absorb([0, 1]))
+        pl.when(jnp.logical_not(both))(lambda: absorb([0]))
+        return
+
+    near = needed(0) | needed(1)
+    far = needed(count - 2) | needed(count - 1)
+    if count > 2:
+        pl.when(near & far)(lambda: absorb(list(range(count))))
+        pl.when(near & jnp.logical_not(far))(lambda: absorb([0, 1]))
+        pl.when(far & jnp.logical_not(near))(lambda: absorb([count - 2, count - 1]))
     else:
-        pl.when(needed)(absorb)
-
-        @pl.when(jnp.logical_not(needed))
-        def _():
-            for n, step in enumerate(steps):
-                finish(n, step, sum_in[n], stat_in[2 * n + 1 : 2 * n + 2, :], stat_in[2 * n : 2 * n + 1, :])
+        pl.when(near)(lambda: absorb([0, 1]))
+
+    @pl.when(jnp.logical_not(near | far))
+    def _():
+        for n, step in enumerate(steps):
+            finish(n, step, sum_in[n], stat_in[2 * n + 1 : 2 * n + 2, :], stat_in[2 * n : 2 * n + 1, :])
+
+    if last:
+        for n in range(len(steps)):
+            leaving(n).wait()
 
 
 def attend(device, lengths, first_queries, second_queries, blocks, sources, state, last):
@@ -182,19 +231,24 @@
     outs = state_shapes
     if last:
         outs = [jax.ShapeDtypeStruct(q.shape, q.dtype) for q in (first_queries, second_queries)]
+    leaving = [pltpu.VMEM(q.shape, q.dtype) for q in (first_queries, second_queries)]
+    leaving.append(pltpu.SemaphoreType.DMA((steps,)))
     return pl.pallas_call(
         functools.partial(attend_kernel, sources, len(blocks), first, last),
         out_shape=outs,
         in_specs=[in_smem, in_smem] + [in_vmem] * (len(operands) - 2),
-        out_specs=[in_vmem] * 2,
-        scratch_shapes=[pltpu.VMEM((keys, width), jnp.float32)],
+        out_specs=[pl.BlockSpec(memory_space=pltpu.HBM) if last else in_vmem] * 2,
+        scratch_shapes=[
+            *(leaving if last else []),
+            pltpu.VMEM((keys, width), jnp.float32),
+        ],
         input_output_aliases=aliases,
         cost_estimate=pl.CostEstimate(
             flops=steps * 4 * keys * width * HEAD_WIDTH,
             bytes_accessed=2 * first_queries.size * 2 + 2 * keys * 2 * KEY_VALUE_HEADS * HEAD_WIDTH,
             transcendentals=steps * keys * width,
         ),
-        compiler_params=pltpu.CompilerParams(vmem_limit_bytes=16 * 1024 * 1024),
+        compiler_params=pltpu.CompilerParams(vmem_limit_bytes=GRANT),
         name="attend_last" if last else "attend",
     )(*operands)
 

time: 50.5 us -> 43.4 us (0.86)
  Pallas kernels: 19.1 us -> 12 us
  starting transfers between devices: 19.1 us -> 18.4 us
  local copies, waits for them, and re-layouts: 3.69 us -> 4.39 us
    pallas_call x4, Pallas kernels: 17.3 us -> 10.9 us  [attend(): pl.pallas_call(functools.partial(attend_kernel, sources, len(blocks), fir...]
    unnamed x10 -> x12, local copies, waits for them, and re-layouts: 3.69 us -> 4.39 us
    ppermute x11, starting transfers between devices: 19.1 us -> 18.4 us  [send(): return lax.ppermute(block, 'seq', route)]
    pallas_call x1, Pallas kernels: 1.82 us -> 1.13 us  [pack(): pl.pallas_call(pack_kernel, out_shape=jax.ShapeDtypeStruct((2 * KEY_VALUE...]
  transfers between devices with their start and end apart: 11 -> 11, of which waited for: 2 -> 2; matrix products, arithmetic and copies ran while one was open for 0% -> 0% of each run, Pallas kernels for 26% -> 17%
where the time goes in v2:
time: 43.4 us; the launch traced here: 43.1 us
  starting transfers between devices  18.4 us (42%)
  Pallas kernels  12 us (28%)
  waiting for transfers between devices  7.35 us (17%)
  local copies, waits for them, and re-layouts  4.39 us (10%)
  between operations  0.93 us (2%)
    ppermute x11, starting transfers between devices, send(): return lax.ppermute(block, 'seq', route)  18.4 us
    pallas_call x4, Pallas kernels, attend(): pl.pallas_call(functools.partial(attend_kernel, sources, len(blocks), fir...  10.9 us
    ppermute x11, waiting for transfers between devices, send(): return lax.ppermute(block, 'seq', route)  7.35 us
    unnamed x12, local copies, waits for them, and re-layouts  4.39 us
    pallas_call x1, Pallas kernels, pack(): pl.pallas_call(pack_kernel, out_shape=jax.ShapeDtypeStruct((2 * KEY_VALUE...  1.13 us
  transfers between devices with their start and end apart: 11, of which 2 were waited for; matrix products, arithmetic and copies ran while one was open for 0% of the time, Pallas kernels for 17%

profile of v2, /device:TPU:17, one launch (start us, length us, event | category | flops | bytes accessed | tf_op | source)
XLA Modules:
  0.0 43.1 jit_solution(10250055135454625872)
XLA Ops:
  0.6 0.0 copy-start.1
  0.6 1.1 %pack.1.refs_4_ = bf16[8,128,128]{2,1,0:T(8,128)(2,1)S(1)} custom-call(bf16[128,512]{1,0:T(8,128)(2,1)} %keys_ref.1, bf16[128,512]{1,0:T(8,128)(2,1)} %values_ref.1), custom_call_target="tpu_custom_call" | custom-call | tf_op jit(solution)/shard_map/pack/pallas_call | solution.py:59
  1.8 3.2 %collective-permute-start = (bf16[8,128,128]{2,1,0:T(8,128)(2,1)S(1)}, bf16[8,128,128]{2,1,0:T(8,128)(2,1)S(1)}, u32[]{:S(2)}, u32[]{:S(2)}) collective-permute-start(bf16[8,128,128]{2,1,0:T(8,128)(2,1)S(1)} %pack.1.refs_4_), channel_id=1, source_target_pairs={{0,4},{1,5},{2,6},{3,7},{4,8},{5,9},{6,10},{7,11},{8,12},{9,13},{1... | collective-permute-start | bytes 786440 | tf_op jit(solution)/shard_map/ppermute | solution.py:262
  5.0 1.0 %collective-permute-start.10 = (bf16[8,128,128]{2,1,0:T(8,128)(2,1)S(1)}, bf16[8,128,128]{2,1,0:T(8,128)(2,1)S(1)}, u32[]{:S(2)}, u32[]{:S(2)}) collective-permute-start(bf16[8,128,128]{2,1,0:T(8,128)(2,1)S(1)} %pack.1.refs_4_), channel_id=1, source_target_pairs={{0,1},{1,0},{2,3},{3,2},{4,5},{5,4},{6,7},{7,6},{8,9},{9,8},{10,11... | collective-permute-start | bytes 786440 | tf_op jit(solution)/shard_map/ppermute | solution.py:262
  6.0 1.2 %collective-permute-start.7 = (bf16[8,128,128]{2,1,0:T(8,128)(2,1)S(1)}, bf16[8,128,128]{2,1,0:T(8,128)(2,1)S(1)}, u32[]{:S(2)}, u32[]{:S(2)}) collective-permute-start(bf16[8,128,128]{2,1,0:T(8,128)(2,1)S(1)} %pack.1.refs_4_), channel_id=1, source_target_pairs={{0,2},{1,3},{2,0},{3,1},{4,6},{5,7},{6,4},{7,5},{8,10},{9,11},{10,... | collective-permute-start | bytes 786440 | tf_op jit(solution)/shard_map/ppermute | solution.py:262
  7.3 3.6 %collective-permute-done.refs_6_ = bf16[8,128,128]{2,1,0:T(8,128)(2,1)S(1)} collective-permute-done((bf16[8,128,128]{2,1,0:T(8,128)(2,1)S(1)}, bf16[8,128,128]{2,1,0:T(8,128)(2,1)S(1)}, u32[]{:S(2)}, u32[]{:S(2)}) %collective-permute-start) | collective-permute-done | bytes 262176 | tf_op jit(solution)/shard_map/ppermute | solution.py:262
  10.9 1.2 %collective-permute-start.3 = (bf16[8,128,128]{2,1,0:T(8,128)(2,1)S(1)}, bf16[8,128,128]{2,1,0:T(8,128)(2,1)S(1)}, u32[]{:S(2)}, u32[]{:S(2)}) collective-permute-start(bf16[8,128,128]{2,1,0:T(8,128)(2,1)S(1)} %collective-permute-done.refs_6_), channel_id=1, source_target_pairs={{0,2},{1,3},{2,0},{3,1},{4,6},{5,7},{6,4},{7,5},{8,10},{9,11},{10,... | collective-permute-start | bytes 786440 | tf_op jit(solution)/shard_map/ppermute | solution.py:262
  12.1 3.2 %collective-permute-start.5 = (bf16[8,128,128]{2,1,0:T(8,128)(2,1)S(1)}, bf16[8,128,128]{2,1,0:T(8,128)(2,1)S(1)}, u32[]{:S(2)}, u32[]{:S(2)}) collective-permute-start(bf16[8,128,128]{2,1,0:T(8,128)(2,1)S(1)} %collective-permute-done.refs_6_), channel_id=1, source_target_pairs={{0,4},{1,5},{2,6},{3,7},{4,8},{5,9},{6,10},{7,11},{8,12},{9,13},{1... | collective-permute-start | bytes 786440 | tf_op jit(solution)/shard_map/ppermute | solution.py:262
  15.3 1.3 %collective-permute-start.1 = (bf16[8,128,128]{2,1,0:T(8,128)(2,1)S(1)}, bf16[8,128,128]{2,1,0:T(8,128)(2,1)S(1)}, u32[]{:S(2)}, u32[]{:S(2)}) collective-permute-start(bf16[8,128,128]{2,1,0:T(8,128)(2,1)S(1)} %collective-permute-done.refs_6_), channel_id=1, source_target_pairs={{2,4},{3,5},{6,8},{7,9},{10,12},{11,13},{18,20},{19,21},{22,24},{2... | collective-permute-start | bytes 786440 | tf_op jit(solution)/shard_map/ppermute | solution.py:262
  16.6 0.0 collective-permute-done.10.refs_5_
  16.6 0.0 copy-start.4
  16.6 0.7 %copy-done.4 = bf16[8,128,128]{2,1,0:T(8,128)(2,1)} copy-done((bf16[8,128,128]{2,1,0:T(8,128)(2,1)}, bf16[8,128,128]{2,1,0:T(8,128)(2,1)S(1)}, u32[]{:S(2)}) %copy-start.4) | copy-done | bytes 262168
  17.3 2.1 %collective-permute-start.9 = (bf16[8,128,128]{2,1,0:T(8,128)(2,1)S(1)}, bf16[8,128,128]{2,1,0:T(8,128)(2,1)S(1)}, u32[]{:S(2)}, u32[]{:S(2)}) collective-permute-start(bf16[8,128,128]{2,1,0:T(8,128)(2,1)S(1)} %collective-permute-done.refs_6_), channel_id=1, source_target_pairs={{0,1},{1,0},{2,3},{3,2},{4,5},{5,4},{6,7},{7,6},{8,9},{9,8},{10,11... | collective-permute-start | bytes 786440 | tf_op jit(solution)/shard_map/ppermute | solution.py:262
  19.4 0.0 collective-permute-done.7.refs_4_
  19.4 0.0 collective-permute-start.8
  19.4 0.0 collective-permute-done.3.refs_4_
  19.4 0.9 %collective-permute-start.4 = (bf16[8,128,128]{2,1,0:T(8,128)(2,1)S(1)}, bf16[8,128,128]{2,1,0:T(8,128)(2,1)S(1)}, u32[]{:S(2)}, u32[]{:S(2)}) collective-permute-start(bf16[8,128,128]{2,1,0:T(8,128)(2,1)S(1)} %collective-permute-done.3.refs_4_), channel_id=1, source_target_pairs={{0,1},{1,0},{2,3},{3,2},{4,5},{5,4},{6,7},{7,6},{8,9},{9,8},{10,11... | collective-permute-start | bytes 786440 | tf_op jit(solution)/shard_map/ppermute | solution.py:262
  20.4 0.0 collective-permute-done.5.refs_6_
  20.4 2.4 %collective-permute-start.6 = (bf16[8,128,128]{2,1,0:T(8,128)(2,1)S(1)}, bf16[8,128,128]{2,1,0:T(8,128)(2,1)S(1)}, u32[]{:S(2)}, u32[]{:S(2)}) collective-permute-start(bf16[8,128,128]{2,1,0:T(8,128)(2,1)S(1)} %collective-permute-done.5.refs_6_), channel_id=1, source_target_pairs={{0,1},{1,0},{2,3},{3,2},{4,5},{5,4},{6,7},{7,6},{8,9},{9,8},{10,11... | collective-permute-start | bytes 786440 | tf_op jit(solution)/shard_map/ppermute | solution.py:262
  22.7 3.7 %collective-permute-done.1.refs_4_ = bf16[8,128,128]{2,1,0:T(8,128)(2,1)S(1)} collective-permute-done((bf16[8,128,128]{2,1,0:T(8,128)(2,1)S(1)}, bf16[8,128,128]{2,1,0:T(8,128)(2,1)S(1)}, u32[]{:S(2)}, u32[]{:S(2)}) %collective-permute-start.1) | collective-permute-done | bytes 262176 | tf_op jit(solution)/shard_map/ppermute | solution.py:262
  26.4 1.8 %collective-permute-start.2 = (bf16[8,128,128]{2,1,0:T(8,128)(2,1)S(1)}, bf16[8,128,128]{2,1,0:T(8,128)(2,1)S(1)}, u32[]{:S(2)}, u32[]{:S(2)}) collective-permute-start(bf16[8,128,128]{2,1,0:T(8,128)(2,1)S(1)} %collective-permute-done.1.refs_4_), channel_id=1, source_target_pairs={{0,1},{1,0},{2,3},{3,2},{4,5},{5,4},{6,7},{7,6},{8,9},{9,8},{10,11... | collective-permute-start | bytes 786440 | tf_op jit(solution)/shard_map/ppermute | solution.py:262
  28.3 1.0 %copy-done = bf16[128,2048]{1,0:T(8,128)(2,1)S(1)} copy-done((bf16[128,2048]{1,0:T(8,128)(2,1)S(1)}, bf16[128,2048]{1,0:T(8,128)(2,1)}, u32[]{:S(2)}) %copy-start) | copy-done | bytes 524312
  29.3 1.0 %copy-done.2 = bf16[128,2048]{1,0:T(8,128)(2,1)S(1)} copy-done((bf16[128,2048]{1,0:T(8,128)(2,1)S(1)}, bf16[128,2048]{1,0:T(8,128)(2,1)}, u32[]{:S(2)}) %copy-start.2) | copy-done | bytes 524312
  30.4 0.7 %copy-done.3 = s32[4]{0:T(128)S(1)} copy-done((s32[4]{0:T(128)S(1)}, s32[4]{0:T(128)}, u32[]{:S(2)}) %copy-start.3) | copy-done | bytes 40
  31.0 0.9 %copy-done.5 = bf16[8,128,128]{2,1,0:T(8,128)(2,1)S(1)} copy-done((bf16[8,128,128]{2,1,0:T(8,128)(2,1)S(1)}, bf16[8,128,128]{2,1,0:T(8,128)(2,1)}, u32[]{:S(2)}) %copy-start.5) | copy-done | bytes 262168
  32.0 2.2 %attend.3 = (f32[16,128,256]{2,1,0:T(8,128)S(1)}, f32[32,256]{1,0:T(8,128)S(1)}) custom-call(s32[1]{0:T(128)} %bitcast.refs_0_, s32[4]{0:T(128)S(1)} %copy-done.3, bf16[128,2048]{1,0:T(8,128)(2,1)S(1)} %copy-done, bf16[128,2048]{1,0:T(8,128)(2,1)S(1)} %copy-done.2, bf16[8,128,128]{2,1,0:T(8,128)(2,1)S(1)} %pack.1.refs_4_, bf16[8,128,128]{2,1,0:T(8,128)(2,1)S(1)} %copy-done.5), custom_call_target="tpu_custom_call" | custom-call | flops 536870912 | bytes 1572864 | tf_op jit(solution)/shard_map/attend/pallas_call | solution.py:236
  34.1 0.0 collective-permute-done.9.refs_7_
  34.2 2.5 %attend.4 = (f32[16,128,256]{2,1,0:T(8,128)S(1)}, f32[32,256]{1,0:T(8,128)S(1)}) custom-call(s32[1]{0:T(128)} %bitcast.refs_0_, s32[4]{0:T(128)S(1)} %copy-done.3, bf16[128,2048]{1,0:T(8,128)(2,1)S(1)} %copy-done.1, bf16[128,2048]{1,0:T(8,128)(2,1)S(1)} %copy-done.2, ...), custom_call_target="tpu_custom_call", output_to_operand_aliasing={{0}: (8, {}), {1}: (9, {})} | custom-call | flops 1073741824 | bytes 2097152 | tf_op jit(solution)/shard_map/attend/pallas_call | solution.py:236
  36.7 0.0 collective-permute-done.4.refs_5_
  36.7 2.7 %attend.5 = (f32[16,128,256]{2,1,0:T(8,128)S(1)}, f32[32,256]{1,0:T(8,128)S(1)}) custom-call(s32[1]{0:T(128)} %bitcast.refs_0_, s32[4]{0:T(128)S(1)} %copy-done.3, bf16[128,2048]{1,0:T(8,128)(2,1)S(1)} %copy-done.1, bf16[128,2048]{1,0:T(8,128)(2,1)S(1)} %copy-done.2, ...), custom_call_target="tpu_custom_call", output_to_operand_aliasing={{0}: (8, {}), {1}: (9, {})} | custom-call | flops 1073741824 | bytes 2097152 | tf_op jit(solution)/shard_map/attend/pallas_call | solution.py:236
  39.5 0.0 collective-permute-done.2.refs_5_
  39.5 3.4 %attend_last.1 = (bf16[128,2048]{1,0:T(8,128)(2,1)}, bf16[128,2048]{1,0:T(8,128)(2,1)}) custom-call(s32[1]{0:T(128)} %bitcast.refs_0_, s32[4]{0:T(128)S(1)} %copy-done.3, bf16[128,2048]{1,0:T(8,128)(2,1)S(1)} %copy-done.1, bf16[128,2048]{1,0:T(8,128)(2,1)S(1)} %copy-done.2, bf16[8,128,128]{2,1,0:T(8,128)(2,1)S(1)} %collective-permute-done.1.refs_4_, ...), custom_call_target="tpu_custom_call" | custom-call | flops 536870912 | bytes 1572864 | tf_op jit(solution)/shard_map/attend_last/pallas_call | solution.py:236
  (7 shorter events, 0.0 us)
Async XLA Ops:
  0.6 33.5 %copy-start.1 = (bf16[128,2048]{1,0:T(8,128)(2,1)S(1)}, bf16[128,2048]{1,0:T(8,128)(2,1)}, u32[]{:S(2)}) copy-start(bf16[128,2048]{1,0:T(8,128)(2,1)} %refs_2_.7) | copy-start | bytes 1572868
  1.8 9.1 %collective-permute-start = (bf16[8,128,128]{2,1,0:T(8,128)(2,1)S(1)}, bf16[8,128,128]{2,1,0:T(8,128)(2,1)S(1)}, u32[]{:S(2)}, u32[]{:S(2)}) collective-permute-start(bf16[8,128,128]{2,1,0:T(8,128)(2,1)S(1)} %pack.1.refs_4_), channel_id=1, source_target_pairs={{0,4},{1,5},{2,6},{3,7},{4,8},{5,9},{6,10},{7,11},{8,12},{9,13},{1... | collective-permute-start | bytes 786440 | tf_op jit(solution)/shard_map/ppermute | solution.py:262
  5.0 11.6 %collective-permute-start.10 = (bf16[8,128,128]{2,1,0:T(8,128)(2,1)S(1)}, bf16[8,128,128]{2,1,0:T(8,128)(2,1)S(1)}, u32[]{:S(2)}, u32[]{:S(2)}) collective-permute-start(bf16[8,128,128]{2,1,0:T(8,128)(2,1)S(1)} %pack.1.refs_4_), channel_id=1, source_target_pairs={{0,1},{1,0},{2,3},{3,2},{4,5},{5,4},{6,7},{7,6},{8,9},{9,8},{10,11... | collective-permute-start | bytes 786440 | tf_op jit(solution)/shard_map/ppermute | solution.py:262
  6.0 13.4 %collective-permute-start.7 = (bf16[8,128,128]{2,1,0:T(8,128)(2,1)S(1)}, bf16[8,128,128]{2,1,0:T(8,128)(2,1)S(1)}, u32[]{:S(2)}, u32[]{:S(2)}) collective-permute-start(bf16[8,128,128]{2,1,0:T(8,128)(2,1)S(1)} %pack.1.refs_4_), channel_id=1, source_target_pairs={{0,2},{1,3},{2,0},{3,1},{4,6},{5,7},{6,4},{7,5},{8,10},{9,11},{10,... | collective-permute-start | bytes 786440 | tf_op jit(solution)/shard_map/ppermute | solution.py:262
  10.9 8.6 %collective-permute-start.3 = (bf16[8,128,128]{2,1,0:T(8,128)(2,1)S(1)}, bf16[8,128,128]{2,1,0:T(8,128)(2,1)S(1)}, u32[]{:S(2)}, u32[]{:S(2)}) collective-permute-start(bf16[8,128,128]{2,1,0:T(8,128)(2,1)S(1)} %collective-permute-done.refs_6_), channel_id=1, source_target_pairs={{0,2},{1,3},{2,0},{3,1},{4,6},{5,7},{6,4},{7,5},{8,10},{9,11},{10,... | collective-permute-start | bytes 786440 | tf_op jit(solution)/shard_map/ppermute | solution.py:262
  12.1 8.3 %collective-permute-start.5 = (bf16[8,128,128]{2,1,0:T(8,128)(2,1)S(1)}, bf16[8,128,128]{2,1,0:T(8,128)(2,1)S(1)}, u32[]{:S(2)}, u32[]{:S(2)}) collective-permute-start(bf16[8,128,128]{2,1,0:T(8,128)(2,1)S(1)} %collective-permute-done.refs_6_), channel_id=1, source_target_pairs={{0,4},{1,5},{2,6},{3,7},{4,8},{5,9},{6,10},{7,11},{8,12},{9,13},{1... | collective-permute-start | bytes 786440 | tf_op jit(solution)/shard_map/ppermute | solution.py:262
  15.3 11.1 %collective-permute-start.1 = (bf16[8,128,128]{2,1,0:T(8,128)(2,1)S(1)}, bf16[8,128,128]{2,1,0:T(8,128)(2,1)S(1)}, u32[]{:S(2)}, u32[]{:S(2)}) collective-permute-start(bf16[8,128,128]{2,1,0:T(8,128)(2,1)S(1)} %collective-permute-done.refs_6_), channel_id=1, source_target_pairs={{2,4},{3,5},{6,8},{7,9},{10,12},{11,13},{18,20},{19,21},{22,24},{2... | collective-permute-start | bytes 786440 | tf_op jit(solution)/shard_map/ppermute | solution.py:262
  16.6 0.7 %copy-start.4 = (bf16[8,128,128]{2,1,0:T(8,128)(2,1)}, bf16[8,128,128]{2,1,0:T(8,128)(2,1)S(1)}, u32[]{:S(2)}) copy-start(bf16[8,128,128]{2,1,0:T(8,128)(2,1)S(1)} %collective-permute-done.10.refs_5_) | copy-start | bytes 786436
  17.3 16.8 %collective-permute-start.9 = (bf16[8,128,128]{2,1,0:T(8,128)(2,1)S(1)}, bf16[8,128,128]{2,1,0:T(8,128)(2,1)S(1)}, u32[]{:S(2)}, u32[]{:S(2)}) collective-permute-start(bf16[8,128,128]{2,1,0:T(8,128)(2,1)S(1)} %collective-permute-done.refs_6_), channel_id=1, source_target_pairs={{0,1},{1,0},{2,3},{3,2},{4,5},{5,4},{6,7},{7,6},{8,9},{9,8},{10,11... | collective-permute-start | bytes 786440 | tf_op jit(solution)/shard_map/ppermute | solution.py:262
  19.4 14.7 %collective-permute-start.8 = (bf16[8,128,128]{2,1,0:T(8,128)(2,1)S(1)}, bf16[8,128,128]{2,1,0:T(8,128)(2,1)S(1)}, u32[]{:S(2)}, u32[]{:S(2)}) collective-permute-start(bf16[8,128,128]{2,1,0:T(8,128)(2,1)S(1)} %collective-permute-done.7.refs_4_), channel_id=1, source_target_pairs={{0,1},{1,0},{2,3},{3,2},{4,5},{5,4},{6,7},{7,6},{8,9},{9,8},{10,11... | collective-permute-start | bytes 786440 | tf_op jit(solution)/shard_map/ppermute | solution.py:262
  19.4 17.3 %collective-permute-start.4 = (bf16[8,128,128]{2,1,0:T(8,128)(2,1)S(1)}, bf16[8,128,128]{2,1,0:T(8,128)(2,1)S(1)}, u32[]{:S(2)}, u32[]{:S(2)}) collective-permute-start(bf16[8,128,128]{2,1,0:T(8,128)(2,1)S(1)} %collective-permute-done.3.refs_4_), channel_id=1, source_target_pairs={{0,1},{1,0},{2,3},{3,2},{4,5},{5,4},{6,7},{7,6},{8,9},{9,8},{10,11... | collective-permute-start | bytes 786440 | tf_op jit(solution)/shard_map/ppermute | solution.py:262
  20.4 16.4 %collective-permute-start.6 = (bf16[8,128,128]{2,1,0:T(8,128)(2,1)S(1)}, bf16[8,128,128]{2,1,0:T(8,128)(2,1)S(1)}, u32[]{:S(2)}, u32[]{:S(2)}) collective-permute-start(bf16[8,128,128]{2,1,0:T(8,128)(2,1)S(1)} %collective-permute-done.5.refs_6_), channel_id=1, source_target_pairs={{0,1},{1,0},{2,3},{3,2},{4,5},{5,4},{6,7},{7,6},{8,9},{9,8},{10,11... | collective-permute-start | bytes 786440 | tf_op jit(solution)/shard_map/ppermute | solution.py:262
  26.4 13.0 %collective-permute-start.2 = (bf16[8,128,128]{2,1,0:T(8,128)(2,1)S(1)}, bf16[8,128,128]{2,1,0:T(8,128)(2,1)S(1)}, u32[]{:S(2)}, u32[]{:S(2)}) collective-permute-start(bf16[8,128,128]{2,1,0:T(8,128)(2,1)S(1)} %collective-permute-done.1.refs_4_), channel_id=1, source_target_pairs={{0,1},{1,0},{2,3},{3,2},{4,5},{5,4},{6,7},{7,6},{8,9},{9,8},{10,11... | collective-permute-start | bytes 786440 | tf_op jit(solution)/shard_map/ppermute | solution.py:262
  28.3 1.0 %copy-start = (bf16[128,2048]{1,0:T(8,128)(2,1)S(1)}, bf16[128,2048]{1,0:T(8,128)(2,1)}, u32[]{:S(2)}) copy-start(bf16[128,2048]{1,0:T(8,128)(2,1)} %refs_2_.7) | copy-start | bytes 1572868
  29.3 1.0 %copy-start.2 = (bf16[128,2048]{1,0:T(8,128)(2,1)S(1)}, bf16[128,2048]{1,0:T(8,128)(2,1)}, u32[]{:S(2)}) copy-start(bf16[128,2048]{1,0:T(8,128)(2,1)} %refs_3_.7) | copy-start | bytes 1572868
  30.4 0.7 %copy-start.3 = (s32[4]{0:T(128)S(1)}, s32[4]{0:T(128)}, u32[]{:S(2)}) copy-start(s32[4]{0:T(128)} %refs_1_.7) | copy-start | bytes 52
  31.0 0.9 %copy-start.5 = (bf16[8,128,128]{2,1,0:T(8,128)(2,1)S(1)}, bf16[8,128,128]{2,1,0:T(8,128)(2,1)}, u32[]{:S(2)}) copy-start(bf16[8,128,128]{2,1,0:T(8,128)(2,1)} %copy-done.4) | copy-start | bytes 786436

commit v3 on v2

--- a/solution.py
+++ b/solution.py
@@ -20,8 +20,9 @@
 HIDDEN = -1e30
 NOWHERE = -(1 << 20)
 PAIR = 2
-AHEAD = 2
 BEHIND = 1
+
+ONES = 16
 
 GRANT = 16 << 20
 SMALL_GRANT = 4 << 20
@@ -32,11 +33,20 @@
 
 
 def shifted(count):
-    return [(d, d + LEVEL) for d in range(count - LEVEL)]
-
-
-def across(count):
-    return [(d, d + LEVEL - ROW) for d in range(count - LEVEL) if d & ROW]
+    return [(d, (d + LEVEL) % count) for d in range(count)]
+
+
+def across(count, held):
+    last = count - LEVEL
+    route = [(d, d ^ ROW) for d in range(held * LEVEL)]
+    for d in range(held * LEVEL, count):
+        if not d & ROW:
+            route.append((d, d + ROW))
+        elif d < last:
+            route.append((d, d + LEVEL - ROW))
+        else:
+            route.append((d, held * LEVEL + d - last - ROW))
+    return route
 
 
 def pack_kernel(keys_ref, values_ref, packed_ref, keys_here, values_here, arrived):
@@ -134,12 +144,13 @@
             highest = jnp.maximum(highest, former)
             fade = jnp.exp2(former - highest)
         weights = jnp.exp2(masked - highest)
-        row_sum = jnp.sum(weights, axis=0, keepdims=True)
-        return n, weights.astype(jnp.bfloat16), highest, fade, row_sum
-
-    def gather(active, n, rounded, highest, fade, row_sum):
+        return n, weights.astype(jnp.bfloat16), highest, fade
+
+    def gather(active, n, rounded, highest, fade):
         values = jnp.concatenate([blocks[i][KEY_VALUE_HEADS + steps[n][0]] for i in active], axis=1)
+        values = jnp.concatenate([values, jnp.ones((ONES, values.shape[1]), values.dtype)], axis=0)
         product = jnp.dot(values, rounded, preferred_element_type=jnp.float32)
+        product, row_sum = product[:HEAD_WIDTH], product[HEAD_WIDTH : HEAD_WIDTH + 1]
         if not first:
             row_sum = row_sum + stat_in[2 * n + 1 : 2 * n + 2, :] * fade
             product = product + sum_in[n] * fade
@@ -155,11 +166,12 @@
             for j in range(PAIR):
                 bias_ref[row * tokens : (row + 1) * tokens, j * tokens : (j + 1) * tokens] = bias
 
-        early = [scores(step, active) for step in steps[:AHEAD]]
+        ahead = 1 if len(active) > 2 else 3
+        early = [scores(step, active) for step in steps[:ahead]]
         late = []
         for n in range(len(steps)):
-            if n + AHEAD < len(steps):
-                early.append(scores(steps[n + AHEAD], active))
+            if n + ahead < len(steps):
+                early.append(scores(steps[n + ahead], active))
             if len(late) > BEHIND:
                 gather(active, *late.pop(0))
             late.append(weigh(n, early.pop(0)))
@@ -275,7 +287,6 @@
 
     own = pack(common_keys, common_values)
     step = functools.partial(attend, device, lengths, first_queries, second_queries)
-
     previous = send(own, shifted(members))
     beside = row(own)
     partner = core(own)
@@ -288,7 +299,7 @@
         following = send(previous, shifted(members))
         over = row(previous)
         if level == rounds - 1:
-            corner = send(previous, across(members))
+            corner = send(previous, across(members, level))
         state = step(blocks, sources, state, False)
         blocks, sources = [over, core(over)], [behind(level, ROW), behind(level, ROW | CORE)]
         previous = following

time: 43.4 us -> 40.7 us (0.938)
  the two profiles are of different devices: /device:TPU:17 before, /device:TPU:11 now
where the time goes in v3:
time: 40.7 us; the launch traced here: 40.4 us
  starting transfers between devices  14.2 us (35%)
  waiting for transfers between devices  10.6 us (26%)
  Pallas kernels  10.3 us (25%)
  local copies, waits for them, and re-layouts  4.4 us (11%)
  between operations  0.89 us (2%)
    ppermute x11, starting transfers between devices, send(): return lax.ppermute(block, 'seq', route)  14.2 us
    ppermute x11, waiting for transfers between devices, send(): return lax.ppermute(block, 'seq', route)  10.6 us
    pallas_call x4, Pallas kernels, attend(): pl.pallas_call(functools.partial(attend_kernel, sources, len(blocks), fir...  9.19 us
    unnamed x12, local copies, waits for them, and re-layouts  4.4 us
    pallas_call x1, Pallas kernels, pack(): pl.pallas_call(pack_kernel, out_shape=jax.ShapeDtypeStruct((2 * KEY_VALUE...  1.13 us
  transfers between devices with their start and end apart: 11, of which 3 were waited for; matrix products, arithmetic and copies ran while one was open for 0% of the time, Pallas kernels for 18%

profile of v3, /device:TPU:11, one launch (start us, length us, event | category | flops | bytes accessed | tf_op | source)
XLA Modules:
  0.0 40.4 jit_solution(15901185766849895990)
XLA Ops:
  0.6 0.0 copy-start.1
  0.6 1.1 %pack.1.refs_4_ = bf16[8,128,128]{2,1,0:T(8,128)(2,1)S(1)} custom-call(bf16[128,512]{1,0:T(8,128)(2,1)} %keys_ref.1, bf16[128,512]{1,0:T(8,128)(2,1)} %values_ref.1), custom_call_target="tpu_custom_call" | custom-call | tf_op jit(solution)/shard_map/pack/pallas_call | solution.py:69
  1.8 1.3 %collective-permute-start = (bf16[8,128,128]{2,1,0:T(8,128)(2,1)S(1)}, bf16[8,128,128]{2,1,0:T(8,128)(2,1)S(1)}, u32[]{:S(2)}, u32[]{:S(2)}) collective-permute-start(bf16[8,128,128]{2,1,0:T(8,128)(2,1)S(1)} %pack.1.refs_4_), channel_id=1, source_target_pairs={{0,4},{1,5},{2,6},{3,7},{4,8},{5,9},{6,10},{7,11},{8,12},{9,13},{1... | collective-permute-start | bytes 786440 | tf_op jit(solution)/shard_map/ppermute | solution.py:274
  3.1 1.0 %collective-permute-start.10 = (bf16[8,128,128]{2,1,0:T(8,128)(2,1)S(1)}, bf16[8,128,128]{2,1,0:T(8,128)(2,1)S(1)}, u32[]{:S(2)}, u32[]{:S(2)}) collective-permute-start(bf16[8,128,128]{2,1,0:T(8,128)(2,1)S(1)} %pack.1.refs_4_), channel_id=1, source_target_pairs={{0,1},{1,0},{2,3},{3,2},{4,5},{5,4},{6,7},{7,6},{8,9},{9,8},{10,11... | collective-permute-start | bytes 786440 | tf_op jit(solution)/shard_map/ppermute | solution.py:274
  4.1 1.2 %collective-permute-start.7 = (bf16[8,128,128]{2,1,0:T(8,128)(2,1)S(1)}, bf16[8,128,128]{2,1,0:T(8,128)(2,1)S(1)}, u32[]{:S(2)}, u32[]{:S(2)}) collective-permute-start(bf16[8,128,128]{2,1,0:T(8,128)(2,1)S(1)} %pack.1.refs_4_), channel_id=1, source_target_pairs={{0,2},{1,3},{2,0},{3,1},{4,6},{5,7},{6,4},{7,5},{8,10},{9,11},{10,... | collective-permute-start | bytes 786440 | tf_op jit(solution)/shard_map/ppermute | solution.py:274
  5.3 3.7 %collective-permute-done.refs_6_ = bf16[8,128,128]{2,1,0:T(8,128)(2,1)S(1)} collective-permute-done((bf16[8,128,128]{2,1,0:T(8,128)(2,1)S(1)}, bf16[8,128,128]{2,1,0:T(8,128)(2,1)S(1)}, u32[]{:S(2)}, u32[]{:S(2)}) %collective-permute-start) | collective-permute-done | bytes 262176 | tf_op jit(solution)/shard_map/ppermute | solution.py:274
  9.0 1.2 %collective-permute-start.3 = (bf16[8,128,128]{2,1,0:T(8,128)(2,1)S(1)}, bf16[8,128,128]{2,1,0:T(8,128)(2,1)S(1)}, u32[]{:S(2)}, u32[]{:S(2)}) collective-permute-start(bf16[8,128,128]{2,1,0:T(8,128)(2,1)S(1)} %collective-permute-done.refs_6_), channel_id=1, source_target_pairs={{0,2},{1,3},{2,0},{3,1},{4,6},{5,7},{6,4},{7,5},{8,10},{9,11},{10,... | collective-permute-start | bytes 786440 | tf_op jit(solution)/shard_map/ppermute | solution.py:274
  10.3 1.3 %collective-permute-start.5 = (bf16[8,128,128]{2,1,0:T(8,128)(2,1)S(1)}, bf16[8,128,128]{2,1,0:T(8,128)(2,1)S(1)}, u32[]{:S(2)}, u32[]{:S(2)}) collective-permute-start(bf16[8,128,128]{2,1,0:T(8,128)(2,1)S(1)} %collective-permute-done.refs_6_), channel_id=1, source_target_pairs={{0,4},{1,5},{2,6},{3,7},{4,8},{5,9},{6,10},{7,11},{8,12},{9,13},{1... | collective-permute-start | bytes 786440 | tf_op jit(solution)/shard_map/ppermute | solution.py:274
  11.6 0.2 collective-permute-start.1
  11.8 0.0 collective-permute-done.10.refs_5_
  11.8 0.7 %copy-done.4 = bf16[8,128,128]{2,1,0:T(8,128)(2,1)} copy-done((bf16[8,128,128]{2,1,0:T(8,128)(2,1)}, bf16[8,128,128]{2,1,0:T(8,128)(2,1)S(1)}, u32[]{:S(2)}) %copy-start.4) | copy-done | bytes 262168
  12.5 2.4 %collective-permute-start.9 = (bf16[8,128,128]{2,1,0:T(8,128)(2,1)S(1)}, bf16[8,128,128]{2,1,0:T(8,128)(2,1)S(1)}, u32[]{:S(2)}, u32[]{:S(2)}) collective-permute-start(bf16[8,128,128]{2,1,0:T(8,128)(2,1)S(1)} %collective-permute-done.refs_6_), channel_id=1, source_target_pairs={{0,1},{1,0},{2,3},{3,2},{4,5},{5,4},{6,7},{7,6},{8,9},{9,8},{10,11... | collective-permute-start | bytes 786440 | tf_op jit(solution)/shard_map/ppermute | solution.py:274
  14.9 0.0 collective-permute-done.7.refs_4_
  14.9 0.0 collective-permute-start.8
  14.9 1.8 %collective-permute-done.3.refs_4_ = bf16[8,128,128]{2,1,0:T(8,128)(2,1)S(1)} collective-permute-done((bf16[8,128,128]{2,1,0:T(8,128)(2,1)S(1)}, bf16[8,128,128]{2,1,0:T(8,128)(2,1)S(1)}, u32[]{:S(2)}, u32[]{:S(2)}) %collective-permute-start.3) | collective-permute-done | bytes 262176 | tf_op jit(solution)/shard_map/ppermute | solution.py:274
  16.7 2.1 %collective-permute-start.4 = (bf16[8,128,128]{2,1,0:T(8,128)(2,1)S(1)}, bf16[8,128,128]{2,1,0:T(8,128)(2,1)S(1)}, u32[]{:S(2)}, u32[]{:S(2)}) collective-permute-start(bf16[8,128,128]{2,1,0:T(8,128)(2,1)S(1)} %collective-permute-done.3.refs_4_), channel_id=1, source_target_pairs={{0,1},{1,0},{2,3},{3,2},{4,5},{5,4},{6,7},{7,6},{8,9},{9,8},{10,11... | collective-permute-start | bytes 786440 | tf_op jit(solution)/shard_map/ppermute | solution.py:274
  18.8 0.0 collective-permute-done.5.refs_6_
  18.8 0.8 %collective-permute-start.6 = (bf16[8,128,128]{2,1,0:T(8,128)(2,1)S(1)}, bf16[8,128,128]{2,1,0:T(8,128)(2,1)S(1)}, u32[]{:S(2)}, u32[]{:S(2)}) collective-permute-start(bf16[8,128,128]{2,1,0:T(8,128)(2,1)S(1)} %collective-permute-done.5.refs_6_), channel_id=1, source_target_pairs={{0,1},{1,0},{2,3},{3,2},{4,5},{5,4},{6,7},{7,6},{8,9},{9,8},{10,11... | collective-permute-start | bytes 786440 | tf_op jit(solution)/shard_map/ppermute | solution.py:274
  19.6 5.0 %collective-permute-done.1.refs_4_ = bf16[8,128,128]{2,1,0:T(8,128)(2,1)S(1)} collective-permute-done((bf16[8,128,128]{2,1,0:T(8,128)(2,1)S(1)}, bf16[8,128,128]{2,1,0:T(8,128)(2,1)S(1)}, u32[]{:S(2)}, u32[]{:S(2)}) %collective-permute-start.1) | collective-permute-done | bytes 262176 | tf_op jit(solution)/shard_map/ppermute | solution.py:274
  24.6 2.6 %collective-permute-start.2 = (bf16[8,128,128]{2,1,0:T(8,128)(2,1)S(1)}, bf16[8,128,128]{2,1,0:T(8,128)(2,1)S(1)}, u32[]{:S(2)}, u32[]{:S(2)}) collective-permute-start(bf16[8,128,128]{2,1,0:T(8,128)(2,1)S(1)} %collective-permute-done.1.refs_4_), channel_id=1, source_target_pairs={{0,1},{1,0},{2,3},{3,2},{4,5},{5,4},{6,7},{7,6},{8,9},{9,8},{10,11... | collective-permute-start | bytes 786440 | tf_op jit(solution)/shard_map/ppermute | solution.py:274
  27.3 1.0 %copy-done = bf16[128,2048]{1,0:T(8,128)(2,1)S(1)} copy-done((bf16[128,2048]{1,0:T(8,128)(2,1)S(1)}, bf16[128,2048]{1,0:T(8,128)(2,1)}, u32[]{:S(2)}) %copy-start) | copy-done | bytes 524312
  28.3 1.0 %copy-done.2 = bf16[128,2048]{1,0:T(8,128)(2,1)S(1)} copy-done((bf16[128,2048]{1,0:T(8,128)(2,1)S(1)}, bf16[128,2048]{1,0:T(8,128)(2,1)}, u32[]{:S(2)}) %copy-start.2) | copy-done | bytes 524312
  29.3 0.7 %copy-done.3 = s32[4]{0:T(128)S(1)} copy-done((s32[4]{0:T(128)S(1)}, s32[4]{0:T(128)}, u32[]{:S(2)}) %copy-start.3) | copy-done | bytes 40
  30.0 0.9 %copy-done.5 = bf16[8,128,128]{2,1,0:T(8,128)(2,1)S(1)} copy-done((bf16[8,128,128]{2,1,0:T(8,128)(2,1)S(1)}, bf16[8,128,128]{2,1,0:T(8,128)(2,1)}, u32[]{:S(2)}) %copy-start.5) | copy-done | bytes 262168
  30.9 2.0 %attend.3 = (f32[16,128,256]{2,1,0:T(8,128)S(1)}, f32[32,256]{1,0:T(8,128)S(1)}) custom-call(s32[1]{0:T(128)} %bitcast.refs_0_, s32[4]{0:T(128)S(1)} %copy-done.3, bf16[128,2048]{1,0:T(8,128)(2,1)S(1)} %copy-done, bf16[128,2048]{1,0:T(8,128)(2,1)S(1)} %copy-done.2, bf16[8,128,128]{2,1,0:T(8,128)(2,1)S(1)} %pack.1.refs_4_, bf16[8,128,128]{2,1,0:T(8,128)(2,1)S(1)} %copy-done.5), custom_call_target="tpu_custom_call" | custom-call | flops 536870912 | bytes 1572864 | tf_op jit(solution)/shard_map/attend/pallas_call | solution.py:248
  33.0 0.0 collective-permute-done.9.refs_7_
  33.0 0.0 collective-permute-done.8.refs_5_
  33.0 2.6 %attend.4 = (f32[16,128,256]{2,1,0:T(8,128)S(1)}, f32[32,256]{1,0:T(8,128)S(1)}) custom-call(s32[1]{0:T(128)} %bitcast.refs_0_, s32[4]{0:T(128)S(1)} %copy-done.3, bf16[128,2048]{1,0:T(8,128)(2,1)S(1)} %copy-done.1, bf16[128,2048]{1,0:T(8,128)(2,1)S(1)} %copy-done.2, ...), custom_call_target="tpu_custom_call", output_to_operand_aliasing={{0}: (8, {}), {1}: (9, {})} | custom-call | flops 1073741824 | bytes 2097152 | tf_op jit(solution)/shard_map/attend/pallas_call | solution.py:248
  35.6 0.0 collective-permute-done.4.refs_5_
  35.7 2.8 %attend.5 = (f32[16,128,256]{2,1,0:T(8,128)S(1)}, f32[32,256]{1,0:T(8,128)S(1)}) custom-call(s32[1]{0:T(128)} %bitcast.refs_0_, s32[4]{0:T(128)S(1)} %copy-done.3, bf16[128,2048]{1,0:T(8,128)(2,1)S(1)} %copy-done.1, bf16[128,2048]{1,0:T(8,128)(2,1)S(1)} %copy-done.2, ...), custom_call_target="tpu_custom_call", output_to_operand_aliasing={{0}: (8, {}), {1}: (9, {})} | custom-call | flops 1073741824 | bytes 2097152 | tf_op jit(solution)/shard_map/attend/pallas_call | solution.py:248
  38.5 0.0 collective-permute-done.2.refs_5_
  38.5 1.7 %attend_last.1 = (bf16[128,2048]{1,0:T(8,128)(2,1)}, bf16[128,2048]{1,0:T(8,128)(2,1)}) custom-call(s32[1]{0:T(128)} %bitcast.refs_0_, s32[4]{0:T(128)S(1)} %copy-done.3, bf16[128,2048]{1,0:T(8,128)(2,1)S(1)} %copy-done.1, bf16[128,2048]{1,0:T(8,128)(2,1)S(1)} %copy-done.2, bf16[8,128,128]{2,1,0:T(8,128)(2,1)S(1)} %collective-permute-done.1.refs_4_, ...), custom_call_target="tpu_custom_call" | custom-call | flops 536870912 | bytes 1572864 | tf_op jit(solution)/shard_map/attend_last/pallas_call | solution.py:248
  (7 shorter events, 0.0 us)
Async XLA Ops:
  0.6 32.4 %copy-start.1 = (bf16[128,2048]{1,0:T(8,128)(2,1)S(1)}, bf16[128,2048]{1,0:T(8,128)(2,1)}, u32[]{:S(2)}) copy-start(bf16[128,2048]{1,0:T(8,128)(2,1)} %refs_2_.7) | copy-start | bytes 1572868
  1.8 7.2 %collective-permute-start = (bf16[8,128,128]{2,1,0:T(8,128)(2,1)S(1)}, bf16[8,128,128]{2,1,0:T(8,128)(2,1)S(1)}, u32[]{:S(2)}, u32[]{:S(2)}) collective-permute-start(bf16[8,128,128]{2,1,0:T(8,128)(2,1)S(1)} %pack.1.refs_4_), channel_id=1, source_target_pairs={{0,4},{1,5},{2,6},{3,7},{4,8},{5,9},{6,10},{7,11},{8,12},{9,13},{1... | collective-permute-start | bytes 786440 | tf_op jit(solution)/shard_map/ppermute | solution.py:274
  3.1 8.7 %collective-permute-start.10 = (bf16[8,128,128]{2,1,0:T(8,128)(2,1)S(1)}, bf16[8,128,128]{2,1,0:T(8,128)(2,1)S(1)}, u32[]{:S(2)}, u32[]{:S(2)}) collective-permute-start(bf16[8,128,128]{2,1,0:T(8,128)(2,1)S(1)} %pack.1.refs_4_), channel_id=1, source_target_pairs={{0,1},{1,0},{2,3},{3,2},{4,5},{5,4},{6,7},{7,6},{8,9},{9,8},{10,11... | collective-permute-start | bytes 786440 | tf_op jit(solution)/shard_map/ppermute | solution.py:274
  4.1 10.8 %collective-permute-start.7 = (bf16[8,128,128]{2,1,0:T(8,128)(2,1)S(1)}, bf16[8,128,128]{2,1,0:T(8,128)(2,1)S(1)}, u32[]{:S(2)}, u32[]{:S(2)}) collective-permute-start(bf16[8,128,128]{2,1,0:T(8,128)(2,1)S(1)} %pack.1.refs_4_), channel_id=1, source_target_pairs={{0,2},{1,3},{2,0},{3,1},{4,6},{5,7},{6,4},{7,5},{8,10},{9,11},{10,... | collective-permute-start | bytes 786440 | tf_op jit(solution)/shard_map/ppermute | solution.py:274
  9.0 7.7 %collective-permute-start.3 = (bf16[8,128,128]{2,1,0:T(8,128)(2,1)S(1)}, bf16[8,128,128]{2,1,0:T(8,128)(2,1)S(1)}, u32[]{:S(2)}, u32[]{:S(2)}) collective-permute-start(bf16[8,128,128]{2,1,0:T(8,128)(2,1)S(1)} %collective-permute-done.refs_6_), channel_id=1, source_target_pairs={{0,2},{1,3},{2,0},{3,1},{4,6},{5,7},{6,4},{7,5},{8,10},{9,11},{10,... | collective-permute-start | bytes 786440 | tf_op jit(solution)/shard_map/ppermute | solution.py:274
  10.3 8.5 %collective-permute-start.5 = (bf16[8,128,128]{2,1,0:T(8,128)(2,1)S(1)}, bf16[8,128,128]{2,1,0:T(8,128)(2,1)S(1)}, u32[]{:S(2)}, u32[]{:S(2)}) collective-permute-start(bf16[8,128,128]{2,1,0:T(8,128)(2,1)S(1)} %collective-permute-done.refs_6_), channel_id=1, source_target_pairs={{0,4},{1,5},{2,6},{3,7},{4,8},{5,9},{6,10},{7,11},{8,12},{9,13},{1... | collective-permute-start | bytes 786440 | tf_op jit(solution)/shard_map/ppermute | solution.py:274
  11.6 13.1 %collective-permute-start.1 = (bf16[8,128,128]{2,1,0:T(8,128)(2,1)S(1)}, bf16[8,128,128]{2,1,0:T(8,128)(2,1)S(1)}, u32[]{:S(2)}, u32[]{:S(2)}) collective-permute-start(bf16[8,128,128]{2,1,0:T(8,128)(2,1)S(1)} %collective-permute-done.refs_6_), channel_id=1, source_target_pairs={{0,2},{1,3},{2,0},{3,1},{4,6},{5,7},{6,8},{7,9},{8,10},{9,11},{10,... | collective-permute-start | bytes 786440 | tf_op jit(solution)/shard_map/ppermute | solution.py:274
  11.8 0.7 %copy-start.4 = (bf16[8,128,128]{2,1,0:T(8,128)(2,1)}, bf16[8,128,128]{2,1,0:T(8,128)(2,1)S(1)}, u32[]{:S(2)}) copy-start(bf16[8,128,128]{2,1,0:T(8,128)(2,1)S(1)} %collective-permute-done.10.refs_5_) | copy-start | bytes 786436
  12.5 20.5 %collective-permute-start.9 = (bf16[8,128,128]{2,1,0:T(8,128)(2,1)S(1)}, bf16[8,128,128]{2,1,0:T(8,128)(2,1)S(1)}, u32[]{:S(2)}, u32[]{:S(2)}) collective-permute-start(bf16[8,128,128]{2,1,0:T(8,128)(2,1)S(1)} %collective-permute-done.refs_6_), channel_id=1, source_target_pairs={{0,1},{1,0},{2,3},{3,2},{4,5},{5,4},{6,7},{7,6},{8,9},{9,8},{10,11... | collective-permute-start | bytes 786440 | tf_op jit(solution)/shard_map/ppermute | solution.py:274
  14.9 18.1 %collective-permute-start.8 = (bf16[8,128,128]{2,1,0:T(8,128)(2,1)S(1)}, bf16[8,128,128]{2,1,0:T(8,128)(2,1)S(1)}, u32[]{:S(2)}, u32[]{:S(2)}) collective-permute-start(bf16[8,128,128]{2,1,0:T(8,128)(2,1)S(1)} %collective-permute-done.7.refs_4_), channel_id=1, source_target_pairs={{0,1},{1,0},{2,3},{3,2},{4,5},{5,4},{6,7},{7,6},{8,9},{9,8},{10,11... | collective-permute-start | bytes 786440 | tf_op jit(solution)/shard_map/ppermute | solution.py:274
  16.7 18.9 %collective-permute-start.4 = (bf16[8,128,128]{2,1,0:T(8,128)(2,1)S(1)}, bf16[8,128,128]{2,1,0:T(8,128)(2,1)S(1)}, u32[]{:S(2)}, u32[]{:S(2)}) collective-permute-start(bf16[8,128,128]{2,1,0:T(8,128)(2,1)S(1)} %collective-permute-done.3.refs_4_), channel_id=1, source_target_pairs={{0,1},{1,0},{2,3},{3,2},{4,5},{5,4},{6,7},{7,6},{8,9},{9,8},{10,11... | collective-permute-start | bytes 786440 | tf_op jit(solution)/shard_map/ppermute | solution.py:274
  18.8 16.9 %collective-permute-start.6 = (bf16[8,128,128]{2,1,0:T(8,128)(2,1)S(1)}, bf16[8,128,128]{2,1,0:T(8,128)(2,1)S(1)}, u32[]{:S(2)}, u32[]{:S(2)}) collective-permute-start(bf16[8,128,128]{2,1,0:T(8,128)(2,1)S(1)} %collective-permute-done.5.refs_6_), channel_id=1, source_target_pairs={{0,1},{1,0},{2,3},{3,2},{4,5},{5,4},{6,7},{7,6},{8,9},{9,8},{10,11... | collective-permute-start | bytes 786440 | tf_op jit(solution)/shard_map/ppermute | solution.py:274
  24.6 13.8 %collective-permute-start.2 = (bf16[8,128,128]{2,1,0:T(8,128)(2,1)S(1)}, bf16[8,128,128]{2,1,0:T(8,128)(2,1)S(1)}, u32[]{:S(2)}, u32[]{:S(2)}) collective-permute-start(bf16[8,128,128]{2,1,0:T(8,128)(2,1)S(1)} %collective-permute-done.1.refs_4_), channel_id=1, source_target_pairs={{0,1},{1,0},{2,3},{3,2},{4,5},{5,4},{6,7},{7,6},{8,9},{9,8},{10,11... | collective-permute-start | bytes 786440 | tf_op jit(solution)/shard_map/ppermute | solution.py:274
  27.3 1.0 %copy-start = (bf16[128,2048]{1,0:T(8,128)(2,1)S(1)}, bf16[128,2048]{1,0:T(8,128)(2,1)}, u32[]{:S(2)}) copy-start(bf16[128,2048]{1,0:T(8,128)(2,1)} %refs_2_.7) | copy-start | bytes 1572868
  28.3 1.0 %copy-start.2 = (bf16[128,2048]{1,0:T(8,128)(2,1)S(1)}, bf16[128,2048]{1,0:T(8,128)(2,1)}, u32[]{:S(2)}) copy-start(bf16[128,2048]{1,0:T(8,128)(2,1)} %refs_3_.7) | copy-start | bytes 1572868
  29.3 0.7 %copy-start.3 = (s32[4]{0:T(128)S(1)}, s32[4]{0:T(128)}, u32[]{:S(2)}) copy-start(s32[4]{0:T(128)} %refs_1_.7) | copy-start | bytes 52
  30.0 0.9 %copy-start.5 = (bf16[8,128,128]{2,1,0:T(8,128)(2,1)S(1)}, bf16[8,128,128]{2,1,0:T(8,128)(2,1)}, u32[]{:S(2)}) copy-start(bf16[8,128,128]{2,1,0:T(8,128)(2,1)} %copy-done.4) | copy-start | bytes 786436

commit v4 on v3

--- a/solution.py
+++ b/solution.py
@@ -81,7 +81,7 @@
     )(*[pltpu.with_memory_space_constraint(a, pltpu.HBM) for a in (keys, values)])
 
 
-def attend_kernel(sources, count, first, last, *refs):
+def attend_kernel(sources, later, count, first, last, *refs):
     refs = list(refs)
     device_ref, lengths_ref, first_ref, second_ref = refs[:4]
     blocks = refs[4 : 4 + count]
@@ -90,11 +90,12 @@
         sum_in, stat_in = rest[:2]
         rest = rest[2:]
     if last:
-        gone_refs, rest = rest[:2], rest[2:]
-        out_refs, left, rest = rest[:2], rest[2], rest[3:]
+        rest = rest[2:]
     else:
         sum_ref, stat_ref = rest[:2]
         rest = rest[2:]
+    if last or later:
+        gone_refs, out_refs, left, rest = rest[:2], rest[2:4], rest[4], rest[5:]
     (bias_ref,) = rest
     if first:
         sum_in, stat_in = None, None
@@ -117,8 +118,11 @@
     bases = [source(device) * tokens for source in sources]
     earliest = start_of(query_base)
 
+    def seen(base):
+        return (base <= query_base + tokens - 1) & (base + tokens - 1 >= earliest)
+
     def needed(i):
-        return (bases[i] <= query_base + tokens - 1) & (bases[i] + tokens - 1 >= earliest)
+        return seen(bases[i])
 
     group = QUERY_HEAD_COUNT // KEY_VALUE_HEADS
     pairs = group // PAIR
@@ -183,15 +187,22 @@
         columns = pl.ds((g * group + pair * PAIR) * HEAD_WIDTH, PAIR * HEAD_WIDTH)
         return pltpu.make_async_copy(out_refs[layer].at[:, columns], gone_refs[layer].at[:, columns], left.at[n])
 
-    def finish(n, step, product, row_sum, highest):
-        g, layer, pair = step
-        if last:
+    def settle(n, step, product, row_sum):
+            g, layer, pair = step
             blended = (product * (1.0 / row_sum)).astype(jnp.bfloat16)
             head = g * group + pair * PAIR
             for i in range(PAIR):
                 columns = slice((head + i) * HEAD_WIDTH, (head + i + 1) * HEAD_WIDTH)
                 out_refs[layer][:, columns] = blended[:, i * tokens : (i + 1) * tokens].T
             leaving(n).start()
+
+    def depart():
+        for n in range(len(steps)):
+            leaving(n).wait()
+
+    def finish(n, step, product, row_sum, highest):
+        if last:
+            settle(n, step, product, row_sum)
         else:
             sum_ref[n] = product
             stat_ref[2 * n : 2 * n + 1, :] = highest
@@ -204,25 +215,36 @@
         return
 
     near = needed(0) | needed(1)
+    if last:
+
+        @pl.when(near)
+        def _():
+            absorb([0, 1])
+            depart()
+
+        return
+
     far = needed(count - 2) | needed(count - 1)
-    if count > 2:
-        pl.when(near & far)(lambda: absorb(list(range(count))))
-        pl.when(near & jnp.logical_not(far))(lambda: absorb([0, 1]))
-        pl.when(far & jnp.logical_not(near))(lambda: absorb([count - 2, count - 1]))
-    else:
-        pl.when(near)(lambda: absorb([0, 1]))
+    pl.when(near & far)(lambda: absorb(list(range(count))))
+    pl.when(near & jnp.logical_not(far))(lambda: absorb([0, 1]))
+    pl.when(far & jnp.logical_not(near))(lambda: absorb([count - 2, count - 1]))
 
     @pl.when(jnp.logical_not(near | far))
     def _():
         for n, step in enumerate(steps):
             finish(n, step, sum_in[n], stat_in[2 * n + 1 : 2 * n + 2, :], stat_in[2 * n : 2 * n + 1, :])
 
-    if last:
-        for n in range(len(steps)):
-            leaving(n).wait()
-
-
-def attend(device, lengths, first_queries, second_queries, blocks, sources, state, last):
+    if later:
+        awaited = functools.reduce(jnp.logical_or, [seen(source(device) * tokens) for source in later])
+
+        @pl.when(jnp.logical_not(awaited))
+        def _():
+            for n, step in enumerate(steps):
+                settle(n, step, sum_ref[n], stat_ref[2 * n + 1 : 2 * n + 2, :])
+            depart()
+
+
+def attend(device, lengths, first_queries, second_queries, blocks, sources, state, later=(), outputs=()):
     tokens = first_queries.shape[0]
     steps = 2 * QUERY_HEAD_COUNT // PAIR
     width = PAIR * tokens
@@ -233,25 +255,30 @@
     in_vmem = pl.BlockSpec(memory_space=pltpu.VMEM)
     in_smem = pl.BlockSpec(memory_space=pltpu.SMEM)
     first = state is None
+    last = bool(outputs)
+    in_hbm = pl.BlockSpec(memory_space=pltpu.HBM)
     operands = [device, lengths, first_queries, second_queries, *blocks]
     aliases = {}
     if not first:
         if not last:
             aliases = {len(operands): 0, len(operands) + 1: 1}
         operands += state
+    if last:
+        aliases = {len(operands): 0, len(operands) + 1: 1}
+        operands += outputs
     keys = len(blocks) * tokens
-    outs = state_shapes
-    if last:
-        outs = [jax.ShapeDtypeStruct(q.shape, q.dtype) for q in (first_queries, second_queries)]
+    outs = [jax.ShapeDtypeStruct(q.shape, q.dtype) for q in (first_queries, second_queries)]
+    if not last:
+        outs = state_shapes + (outs if later else [])
     leaving = [pltpu.VMEM(q.shape, q.dtype) for q in (first_queries, second_queries)]
     leaving.append(pltpu.SemaphoreType.DMA((steps,)))
     return pl.pallas_call(
-        functools.partial(attend_kernel, sources, len(blocks), first, last),
+        functools.partial(attend_kernel, sources, later, len(blocks), first, last),
         out_shape=outs,
-        in_specs=[in_smem, in_smem] + [in_vmem] * (len(operands) - 2),
-        out_specs=[pl.BlockSpec(memory_space=pltpu.HBM) if last else in_vmem] * 2,
+        in_specs=[in_smem, in_smem] + [in_vmem] * (len(operands) - 2 - len(outputs)) + [in_hbm] * len(outputs),
+        out_specs=[in_hbm] * 2 if last else [in_vmem] * 2 + [in_hbm] * (len(outs) - 2),
         scratch_shapes=[
-            *(leaving if last else []),
+            *(leaving if last or later else []),
             pltpu.VMEM((keys, width), jnp.float32),
         ],
         input_output_aliases=aliases,
@@ -290,7 +317,7 @@
     previous = send(own, shifted(members))
     beside = row(own)
     partner = core(own)
-    state = step([own, partner], [behind(0, 0), behind(0, CORE)], None, False)
+    state = step([own, partner], [behind(0, 0), behind(0, CORE)], None)
 
     blocks, sources = [beside, core(beside)], [behind(0, ROW), behind(0, ROW | CORE)]
     for level in range(1, rounds):
@@ -300,20 +327,15 @@
         over = row(previous)
         if level == rounds - 1:
             corner = send(previous, across(members, level))
-        state = step(blocks, sources, state, False)
+        state = step(blocks, sources, state)
         blocks, sources = [over, core(over)], [behind(level, ROW), behind(level, ROW | CORE)]
         previous = following
     blocks += [previous, core(previous)]
     sources += [behind(rounds, 0), behind(rounds, CORE)]
-    state = step(blocks, sources, state, False)
-    return tuple(
-        step(
-            [corner, core(corner)],
-            [upper_behind(rounds, ROW), upper_behind(rounds, ROW | CORE)],
-            state,
-            True,
-        )
-    )
+    later = [upper_behind(rounds, ROW), upper_behind(rounds, ROW | CORE)]
+    *state, first_output, second_output = step(blocks, sources, state, later)
+    blocks = [corner, core(corner)]
+    return tuple(step(blocks, later, state, outputs=[first_output, second_output]))
 
 
 def solution(mesh):

time: 40.7 us -> 40.8 us (level)
  transfers between devices with their start and end apart: 11 -> 11, of which waited for: 3 -> 3; matrix products, arithmetic and copies ran while one was open for 0% -> 0% of each run, Pallas kernels for 18% -> 21%
where the time goes in v4:
time: 40.8 us; the launch traced here: 40.5 us
  starting transfers between devices  14.2 us (35%)
  waiting for transfers between devices  10.6 us (26%)
  Pallas kernels  10.5 us (26%)
  local copies, waits for them, and re-layouts  4.4 us (11%)
  between operations  0.89 us (2%)
    ppermute x11, starting transfers between devices, send(): return lax.ppermute(block, 'seq', route)  14.2 us
    ppermute x11, waiting for transfers between devices, send(): return lax.ppermute(block, 'seq', route)  10.6 us
    pallas_call x4, Pallas kernels, attend(): pl.pallas_call(functools.partial(attend_kernel, sources, later, len(block...  9.35 us
    unnamed x12, local copies, waits for them, and re-layouts  4.4 us
    pallas_call x1, Pallas kernels, pack(): pl.pallas_call(pack_kernel, out_shape=jax.ShapeDtypeStruct((2 * KEY_VALUE...  1.13 us
  transfers between devices with their start and end apart: 11, of which 3 were waited for; matrix products, arithmetic and copies ran while one was open for 0% of the time, Pallas kernels for 21%

profile of v4, /device:TPU:11, one launch (start us, length us, event | category | flops | bytes accessed | tf_op | source)
XLA Modules:
  0.0 40.5 jit_solution(17450636385610172176)
XLA Ops:
  0.6 0.0 copy-start.1
  0.6 1.1 %pack.1.refs_4_ = bf16[8,128,128]{2,1,0:T(8,128)(2,1)S(1)} custom-call(bf16[128,512]{1,0:T(8,128)(2,1)} %keys_ref.1, bf16[128,512]{1,0:T(8,128)(2,1)} %values_ref.1), custom_call_target="tpu_custom_call" | custom-call | tf_op jit(solution)/shard_map/pack/pallas_call | solution.py:69
  1.8 1.3 %collective-permute-start = (bf16[8,128,128]{2,1,0:T(8,128)(2,1)S(1)}, bf16[8,128,128]{2,1,0:T(8,128)(2,1)S(1)}, u32[]{:S(2)}, u32[]{:S(2)}) collective-permute-start(bf16[8,128,128]{2,1,0:T(8,128)(2,1)S(1)} %pack.1.refs_4_), channel_id=1, source_target_pairs={{0,4},{1,5},{2,6},{3,7},{4,8},{5,9},{6,10},{7,11},{8,12},{9,13},{1... | collective-permute-start | bytes 786440 | tf_op jit(solution)/shard_map/ppermute | solution.py:301
  3.1 1.0 %collective-permute-start.10 = (bf16[8,128,128]{2,1,0:T(8,128)(2,1)S(1)}, bf16[8,128,128]{2,1,0:T(8,128)(2,1)S(1)}, u32[]{:S(2)}, u32[]{:S(2)}) collective-permute-start(bf16[8,128,128]{2,1,0:T(8,128)(2,1)S(1)} %pack.1.refs_4_), channel_id=1, source_target_pairs={{0,1},{1,0},{2,3},{3,2},{4,5},{5,4},{6,7},{7,6},{8,9},{9,8},{10,11... | collective-permute-start | bytes 786440 | tf_op jit(solution)/shard_map/ppermute | solution.py:301
  4.1 1.2 %collective-permute-start.7 = (bf16[8,128,128]{2,1,0:T(8,128)(2,1)S(1)}, bf16[8,128,128]{2,1,0:T(8,128)(2,1)S(1)}, u32[]{:S(2)}, u32[]{:S(2)}) collective-permute-start(bf16[8,128,128]{2,1,0:T(8,128)(2,1)S(1)} %pack.1.refs_4_), channel_id=1, source_target_pairs={{0,2},{1,3},{2,0},{3,1},{4,6},{5,7},{6,4},{7,5},{8,10},{9,11},{10,... | collective-permute-start | bytes 786440 | tf_op jit(solution)/shard_map/ppermute | solution.py:301
  5.3 3.7 %collective-permute-done.refs_6_ = bf16[8,128,128]{2,1,0:T(8,128)(2,1)S(1)} collective-permute-done((bf16[8,128,128]{2,1,0:T(8,128)(2,1)S(1)}, bf16[8,128,128]{2,1,0:T(8,128)(2,1)S(1)}, u32[]{:S(2)}, u32[]{:S(2)}) %collective-permute-start) | collective-permute-done | bytes 262176 | tf_op jit(solution)/shard_map/ppermute | solution.py:301
  9.0 1.2 %collective-permute-start.3 = (bf16[8,128,128]{2,1,0:T(8,128)(2,1)S(1)}, bf16[8,128,128]{2,1,0:T(8,128)(2,1)S(1)}, u32[]{:S(2)}, u32[]{:S(2)}) collective-permute-start(bf16[8,128,128]{2,1,0:T(8,128)(2,1)S(1)} %collective-permute-done.refs_6_), channel_id=1, source_target_pairs={{0,2},{1,3},{2,0},{3,1},{4,6},{5,7},{6,4},{7,5},{8,10},{9,11},{10,... | collective-permute-start | bytes 786440 | tf_op jit(solution)/shard_map/ppermute | solution.py:301
  10.3 1.3 %collective-permute-start.5 = (bf16[8,128,128]{2,1,0:T(8,128)(2,1)S(1)}, bf16[8,128,128]{2,1,0:T(8,128)(2,1)S(1)}, u32[]{:S(2)}, u32[]{:S(2)}) collective-permute-start(bf16[8,128,128]{2,1,0:T(8,128)(2,1)S(1)} %collective-permute-done.refs_6_), channel_id=1, source_target_pairs={{0,4},{1,5},{2,6},{3,7},{4,8},{5,9},{6,10},{7,11},{8,12},{9,13},{1... | collective-permute-start | bytes 786440 | tf_op jit(solution)/shard_map/ppermute | solution.py:301
  11.6 0.2 collective-permute-start.1
  11.8 0.0 collective-permute-done.10.refs_5_
  11.8 0.7 %copy-done.4 = bf16[8,128,128]{2,1,0:T(8,128)(2,1)} copy-done((bf16[8,128,128]{2,1,0:T(8,128)(2,1)}, bf16[8,128,128]{2,1,0:T(8,128)(2,1)S(1)}, u32[]{:S(2)}) %copy-start.4) | copy-done | bytes 262168
  12.5 2.4 %collective-permute-start.9 = (bf16[8,128,128]{2,1,0:T(8,128)(2,1)S(1)}, bf16[8,128,128]{2,1,0:T(8,128)(2,1)S(1)}, u32[]{:S(2)}, u32[]{:S(2)}) collective-permute-start(bf16[8,128,128]{2,1,0:T(8,128)(2,1)S(1)} %collective-permute-done.refs_6_), channel_id=1, source_target_pairs={{0,1},{1,0},{2,3},{3,2},{4,5},{5,4},{6,7},{7,6},{8,9},{9,8},{10,11... | collective-permute-start | bytes 786440 | tf_op jit(solution)/shard_map/ppermute | solution.py:301
  14.9 0.0 collective-permute-done.7.refs_4_
  14.9 0.0 collective-permute-start.8
  14.9 1.8 %collective-permute-done.3.refs_4_ = bf16[8,128,128]{2,1,0:T(8,128)(2,1)S(1)} collective-permute-done((bf16[8,128,128]{2,1,0:T(8,128)(2,1)S(1)}, bf16[8,128,128]{2,1,0:T(8,128)(2,1)S(1)}, u32[]{:S(2)}, u32[]{:S(2)}) %collective-permute-start.3) | collective-permute-done | bytes 262176 | tf_op jit(solution)/shard_map/ppermute | solution.py:301
  16.7 2.1 %collective-permute-start.4 = (bf16[8,128,128]{2,1,0:T(8,128)(2,1)S(1)}, bf16[8,128,128]{2,1,0:T(8,128)(2,1)S(1)}, u32[]{:S(2)}, u32[]{:S(2)}) collective-permute-start(bf16[8,128,128]{2,1,0:T(8,128)(2,1)S(1)} %collective-permute-done.3.refs_4_), channel_id=1, source_target_pairs={{0,1},{1,0},{2,3},{3,2},{4,5},{5,4},{6,7},{7,6},{8,9},{9,8},{10,11... | collective-permute-start | bytes 786440 | tf_op jit(solution)/shard_map/ppermute | solution.py:301
  18.8 0.0 collective-permute-done.5.refs_6_
  18.8 0.8 %collective-permute-start.6 = (bf16[8,128,128]{2,1,0:T(8,128)(2,1)S(1)}, bf16[8,128,128]{2,1,0:T(8,128)(2,1)S(1)}, u32[]{:S(2)}, u32[]{:S(2)}) collective-permute-start(bf16[8,128,128]{2,1,0:T(8,128)(2,1)S(1)} %collective-permute-done.5.refs_6_), channel_id=1, source_target_pairs={{0,1},{1,0},{2,3},{3,2},{4,5},{5,4},{6,7},{7,6},{8,9},{9,8},{10,11... | collective-permute-start | bytes 786440 | tf_op jit(solution)/shard_map/ppermute | solution.py:301
  19.6 5.0 %collective-permute-done.1.refs_4_ = bf16[8,128,128]{2,1,0:T(8,128)(2,1)S(1)} collective-permute-done((bf16[8,128,128]{2,1,0:T(8,128)(2,1)S(1)}, bf16[8,128,128]{2,1,0:T(8,128)(2,1)S(1)}, u32[]{:S(2)}, u32[]{:S(2)}) %collective-permute-start.1) | collective-permute-done | bytes 262176 | tf_op jit(solution)/shard_map/ppermute | solution.py:301
  24.6 2.6 %collective-permute-start.2 = (bf16[8,128,128]{2,1,0:T(8,128)(2,1)S(1)}, bf16[8,128,128]{2,1,0:T(8,128)(2,1)S(1)}, u32[]{:S(2)}, u32[]{:S(2)}) collective-permute-start(bf16[8,128,128]{2,1,0:T(8,128)(2,1)S(1)} %collective-permute-done.1.refs_4_), channel_id=1, source_target_pairs={{0,1},{1,0},{2,3},{3,2},{4,5},{5,4},{6,7},{7,6},{8,9},{9,8},{10,11... | collective-permute-start | bytes 786440 | tf_op jit(solution)/shard_map/ppermute | solution.py:301
  27.3 1.0 %copy-done = bf16[128,2048]{1,0:T(8,128)(2,1)S(1)} copy-done((bf16[128,2048]{1,0:T(8,128)(2,1)S(1)}, bf16[128,2048]{1,0:T(8,128)(2,1)}, u32[]{:S(2)}) %copy-start) | copy-done | bytes 524312
  28.3 1.0 %copy-done.2 = bf16[128,2048]{1,0:T(8,128)(2,1)S(1)} copy-done((bf16[128,2048]{1,0:T(8,128)(2,1)S(1)}, bf16[128,2048]{1,0:T(8,128)(2,1)}, u32[]{:S(2)}) %copy-start.2) | copy-done | bytes 524312
  29.3 0.7 %copy-done.3 = s32[4]{0:T(128)S(1)} copy-done((s32[4]{0:T(128)S(1)}, s32[4]{0:T(128)}, u32[]{:S(2)}) %copy-start.3) | copy-done | bytes 40
  30.0 0.9 %copy-done.5 = bf16[8,128,128]{2,1,0:T(8,128)(2,1)S(1)} copy-done((bf16[8,128,128]{2,1,0:T(8,128)(2,1)S(1)}, bf16[8,128,128]{2,1,0:T(8,128)(2,1)}, u32[]{:S(2)}) %copy-start.5) | copy-done | bytes 262168
  30.9 2.0 %attend.3 = (f32[16,128,256]{2,1,0:T(8,128)S(1)}, f32[32,256]{1,0:T(8,128)S(1)}) custom-call(s32[1]{0:T(128)} %bitcast.refs_0_, s32[4]{0:T(128)S(1)} %copy-done.3, bf16[128,2048]{1,0:T(8,128)(2,1)S(1)} %copy-done, bf16[128,2048]{1,0:T(8,128)(2,1)S(1)} %copy-done.2, bf16[8,128,128]{2,1,0:T(8,128)(2,1)S(1)} %pack.1.refs_4_, bf16[8,128,128]{2,1,0:T(8,128)(2,1)S(1)} %copy-done.5), custom_call_target="tpu_custom_call" | custom-call | flops 536870912 | bytes 1572864 | tf_op jit(solution)/shard_map/attend/pallas_call | solution.py:275
  33.0 0.0 collective-permute-done.9.refs_7_
  33.0 0.0 collective-permute-done.8.refs_5_
  33.0 2.6 %attend.4 = (f32[16,128,256]{2,1,0:T(8,128)S(1)}, f32[32,256]{1,0:T(8,128)S(1)}) custom-call(s32[1]{0:T(128)} %bitcast.refs_0_, s32[4]{0:T(128)S(1)} %copy-done.3, bf16[128,2048]{1,0:T(8,128)(2,1)S(1)} %copy-done.1, bf16[128,2048]{1,0:T(8,128)(2,1)S(1)} %copy-done.2, ...), custom_call_target="tpu_custom_call", output_to_operand_aliasing={{0}: (8, {}), {1}: (9, {})} | custom-call | flops 1073741824 | bytes 2097152 | tf_op jit(solution)/shard_map/attend/pallas_call | solution.py:275
  35.6 0.0 collective-permute-done.4.refs_5_
  35.7 0.0 collective-permute-done.6.refs_7_
  35.7 4.0 %attend.5 = (f32[16,128,256]{2,1,0:T(8,128)S(1)}, f32[32,256]{1,0:T(8,128)S(1)}, bf16[128,2048]{1,0:T(8,128)(2,1)}, bf16[128,2048]{1,0:T(8,128)(2,1)}) custom-call(s32[1]{0:T(128)} %bitcast.refs_0_, s32[4]{0:T(128)S(1)} %copy-done.3, bf16[128,2048]{1,0:T(8,128)(2,1)S(1)} %copy-done.1, ...), custom_call_target="tpu_custom_call", output_to_operand_aliasing={{0}: (8, {}), {1}: (9, {})} | custom-call | flops 1073741824 | bytes 2097152 | tf_op jit(solution)/shard_map/attend/pallas_call | solution.py:275
  39.7 0.7 %attend_last.1 = (bf16[128,2048]{1,0:T(8,128)(2,1)}, bf16[128,2048]{1,0:T(8,128)(2,1)}) custom-call(s32[1]{0:T(128)} %bitcast.refs_0_, s32[4]{0:T(128)S(1)} %copy-done.3, bf16[128,2048]{1,0:T(8,128)(2,1)S(1)} %copy-done.1, bf16[128,2048]{1,0:T(8,128)(2,1)S(1)} %copy-done.2, ...), custom_call_target="tpu_custom_call", output_to_operand_aliasing={{0}: (8, {}), {1}: (9, {})} | custom-call | flops 536870912 | bytes 1572864 | tf_op jit(solution)/shard_map/attend_last/pallas_call | solution.py:275
  (7 shorter events, 0.0 us)
Async XLA Ops:
  0.6 32.4 %copy-start.1 = (bf16[128,2048]{1,0:T(8,128)(2,1)S(1)}, bf16[128,2048]{1,0:T(8,128)(2,1)}, u32[]{:S(2)}) copy-start(bf16[128,2048]{1,0:T(8,128)(2,1)} %refs_2_.7) | copy-start | bytes 1572868
  1.8 7.2 %collective-permute-start = (bf16[8,128,128]{2,1,0:T(8,128)(2,1)S(1)}, bf16[8,128,128]{2,1,0:T(8,128)(2,1)S(1)}, u32[]{:S(2)}, u32[]{:S(2)}) collective-permute-start(bf16[8,128,128]{2,1,0:T(8,128)(2,1)S(1)} %pack.1.refs_4_), channel_id=1, source_target_pairs={{0,4},{1,5},{2,6},{3,7},{4,8},{5,9},{6,10},{7,11},{8,12},{9,13},{1... | collective-permute-start | bytes 786440 | tf_op jit(solution)/shard_map/ppermute | solution.py:301
  3.1 8.7 %collective-permute-start.10 = (bf16[8,128,128]{2,1,0:T(8,128)(2,1)S(1)}, bf16[8,128,128]{2,1,0:T(8,128)(2,1)S(1)}, u32[]{:S(2)}, u32[]{:S(2)}) collective-permute-start(bf16[8,128,128]{2,1,0:T(8,128)(2,1)S(1)} %pack.1.refs_4_), channel_id=1, source_target_pairs={{0,1},{1,0},{2,3},{3,2},{4,5},{5,4},{6,7},{7,6},{8,9},{9,8},{10,11... | collective-permute-start | bytes 786440 | tf_op jit(solution)/shard_map/ppermute | solution.py:301
  4.1 10.8 %collective-permute-start.7 = (bf16[8,128,128]{2,1,0:T(8,128)(2,1)S(1)}, bf16[8,128,128]{2,1,0:T(8,128)(2,1)S(1)}, u32[]{:S(2)}, u32[]{:S(2)}) collective-permute-start(bf16[8,128,128]{2,1,0:T(8,128)(2,1)S(1)} %pack.1.refs_4_), channel_id=1, source_target_pairs={{0,2},{1,3},{2,0},{3,1},{4,6},{5,7},{6,4},{7,5},{8,10},{9,11},{10,... | collective-permute-start | bytes 786440 | tf_op jit(solution)/shard_map/ppermute | solution.py:301
  9.0 7.7 %collective-permute-start.3 = (bf16[8,128,128]{2,1,0:T(8,128)(2,1)S(1)}, bf16[8,128,128]{2,1,0:T(8,128)(2,1)S(1)}, u32[]{:S(2)}, u32[]{:S(2)}) collective-permute-start(bf16[8,128,128]{2,1,0:T(8,128)(2,1)S(1)} %collective-permute-done.refs_6_), channel_id=1, source_target_pairs={{0,2},{1,3},{2,0},{3,1},{4,6},{5,7},{6,4},{7,5},{8,10},{9,11},{10,... | collective-permute-start | bytes 786440 | tf_op jit(solution)/shard_map/ppermute | solution.py:301
  10.3 8.5 %collective-permute-start.5 = (bf16[8,128,128]{2,1,0:T(8,128)(2,1)S(1)}, bf16[8,128,128]{2,1,0:T(8,128)(2,1)S(1)}, u32[]{:S(2)}, u32[]{:S(2)}) collective-permute-start(bf16[8,128,128]{2,1,0:T(8,128)(2,1)S(1)} %collective-permute-done.refs_6_), channel_id=1, source_target_pairs={{0,4},{1,5},{2,6},{3,7},{4,8},{5,9},{6,10},{7,11},{8,12},{9,13},{1... | collective-permute-start | bytes 786440 | tf_op jit(solution)/shard_map/ppermute | solution.py:301
  11.6 13.1 %collective-permute-start.1 = (bf16[8,128,128]{2,1,0:T(8,128)(2,1)S(1)}, bf16[8,128,128]{2,1,0:T(8,128)(2,1)S(1)}, u32[]{:S(2)}, u32[]{:S(2)}) collective-permute-start(bf16[8,128,128]{2,1,0:T(8,128)(2,1)S(1)} %collective-permute-done.refs_6_), channel_id=1, source_target_pairs={{0,2},{1,3},{2,0},{3,1},{4,6},{5,7},{6,8},{7,9},{8,10},{9,11},{10,... | collective-permute-start | bytes 786440 | tf_op jit(solution)/shard_map/ppermute | solution.py:301
  11.8 0.7 %copy-start.4 = (bf16[8,128,128]{2,1,0:T(8,128)(2,1)}, bf16[8,128,128]{2,1,0:T(8,128)(2,1)S(1)}, u32[]{:S(2)}) copy-start(bf16[8,128,128]{2,1,0:T(8,128)(2,1)S(1)} %collective-permute-done.10.refs_5_) | copy-start | bytes 786436
  12.5 20.5 %collective-permute-start.9 = (bf16[8,128,128]{2,1,0:T(8,128)(2,1)S(1)}, bf16[8,128,128]{2,1,0:T(8,128)(2,1)S(1)}, u32[]{:S(2)}, u32[]{:S(2)}) collective-permute-start(bf16[8,128,128]{2,1,0:T(8,128)(2,1)S(1)} %collective-permute-done.refs_6_), channel_id=1, source_target_pairs={{0,1},{1,0},{2,3},{3,2},{4,5},{5,4},{6,7},{7,6},{8,9},{9,8},{10,11... | collective-permute-start | bytes 786440 | tf_op jit(solution)/shard_map/ppermute | solution.py:301
  14.9 18.1 %collective-permute-start.8 = (bf16[8,128,128]{2,1,0:T(8,128)(2,1)S(1)}, bf16[8,128,128]{2,1,0:T(8,128)(2,1)S(1)}, u32[]{:S(2)}, u32[]{:S(2)}) collective-permute-start(bf16[8,128,128]{2,1,0:T(8,128)(2,1)S(1)} %collective-permute-done.7.refs_4_), channel_id=1, source_target_pairs={{0,1},{1,0},{2,3},{3,2},{4,5},{5,4},{6,7},{7,6},{8,9},{9,8},{10,11... | collective-permute-start | bytes 786440 | tf_op jit(solution)/shard_map/ppermute | solution.py:301
  16.7 18.9 %collective-permute-start.4 = (bf16[8,128,128]{2,1,0:T(8,128)(2,1)S(1)}, bf16[8,128,128]{2,1,0:T(8,128)(2,1)S(1)}, u32[]{:S(2)}, u32[]{:S(2)}) collective-permute-start(bf16[8,128,128]{2,1,0:T(8,128)(2,1)S(1)} %collective-permute-done.3.refs_4_), channel_id=1, source_target_pairs={{0,1},{1,0},{2,3},{3,2},{4,5},{5,4},{6,7},{7,6},{8,9},{9,8},{10,11... | collective-permute-start | bytes 786440 | tf_op jit(solution)/shard_map/ppermute | solution.py:301
  18.8 16.9 %collective-permute-start.6 = (bf16[8,128,128]{2,1,0:T(8,128)(2,1)S(1)}, bf16[8,128,128]{2,1,0:T(8,128)(2,1)S(1)}, u32[]{:S(2)}, u32[]{:S(2)}) collective-permute-start(bf16[8,128,128]{2,1,0:T(8,128)(2,1)S(1)} %collective-permute-done.5.refs_6_), channel_id=1, source_target_pairs={{0,1},{1,0},{2,3},{3,2},{4,5},{5,4},{6,7},{7,6},{8,9},{9,8},{10,11... | collective-permute-start | bytes 786440 | tf_op jit(solution)/shard_map/ppermute | solution.py:301
  24.6 15.0 %collective-permute-start.2 = (bf16[8,128,128]{2,1,0:T(8,128)(2,1)S(1)}, bf16[8,128,128]{2,1,0:T(8,128)(2,1)S(1)}, u32[]{:S(2)}, u32[]{:S(2)}) collective-permute-start(bf16[8,128,128]{2,1,0:T(8,128)(2,1)S(1)} %collective-permute-done.1.refs_4_), channel_id=1, source_target_pairs={{0,1},{1,0},{2,3},{3,2},{4,5},{5,4},{6,7},{7,6},{8,9},{9,8},{10,11... | collective-permute-start | bytes 786440 | tf_op jit(solution)/shard_map/ppermute | solution.py:301
  27.3 1.0 %copy-start = (bf16[128,2048]{1,0:T(8,128)(2,1)S(1)}, bf16[128,2048]{1,0:T(8,128)(2,1)}, u32[]{:S(2)}) copy-start(bf16[128,2048]{1,0:T(8,128)(2,1)} %refs_2_.7) | copy-start | bytes 1572868
  28.3 1.0 %copy-start.2 = (bf16[128,2048]{1,0:T(8,128)(2,1)S(1)}, bf16[128,2048]{1,0:T(8,128)(2,1)}, u32[]{:S(2)}) copy-start(bf16[128,2048]{1,0:T(8,128)(2,1)} %refs_3_.7) | copy-start | bytes 1572868
  29.3 0.7 %copy-start.3 = (s32[4]{0:T(128)S(1)}, s32[4]{0:T(128)}, u32[]{:S(2)}) copy-start(s32[4]{0:T(128)} %refs_1_.7) | copy-start | bytes 52
  30.0 0.9 %copy-start.5 = (bf16[8,128,128]{2,1,0:T(8,128)(2,1)S(1)}, bf16[8,128,128]{2,1,0:T(8,128)(2,1)}, u32[]{:S(2)}) copy-start(bf16[8,128,128]{2,1,0:T(8,128)(2,1)} %copy-done.4) | copy-start | bytes 786436

commit v5 on v4

--- a/solution.py
+++ b/solution.py
@@ -229,19 +229,28 @@
     pl.when(near & jnp.logical_not(far))(lambda: absorb([0, 1]))
     pl.when(far & jnp.logical_not(near))(lambda: absorb([count - 2, count - 1]))
 
-    @pl.when(jnp.logical_not(near | far))
-    def _():
-        for n, step in enumerate(steps):
-            finish(n, step, sum_in[n], stat_in[2 * n + 1 : 2 * n + 2, :], stat_in[2 * n : 2 * n + 1, :])
-
+    kept = jnp.logical_not(near | far)
     if later:
         awaited = functools.reduce(jnp.logical_or, [seen(source(device) * tokens) for source in later])
 
-        @pl.when(jnp.logical_not(awaited))
+        @pl.when(jnp.logical_not(kept | awaited))
         def _():
             for n, step in enumerate(steps):
                 settle(n, step, sum_ref[n], stat_ref[2 * n + 1 : 2 * n + 2, :])
             depart()
+
+        @pl.when(kept & jnp.logical_not(awaited))
+        def _():
+            for n, step in enumerate(steps):
+                settle(n, step, sum_in[n], stat_in[2 * n + 1 : 2 * n + 2, :])
+            depart()
+
+        kept = kept & awaited
+
+    @pl.when(kept)
+    def _():
+        for n, step in enumerate(steps):
+            finish(n, step, sum_in[n], stat_in[2 * n + 1 : 2 * n + 2, :], stat_in[2 * n : 2 * n + 1, :])
 
 
 def attend(device, lengths, first_queries, second_queries, blocks, sources, state, later=(), outputs=()):

time: 40.8 us -> 40.8 us (level)
  no operation moved by 1% of the time
where the time goes in v5:
time: 40.8 us; the launch traced here: 40.5 us
  starting transfers between devices  14.2 us (35%)
  waiting for transfers between devices  10.6 us (26%)
  Pallas kernels  10.5 us (26%)
  local copies, waits for them, and re-layouts  4.4 us (11%)
  between operations  0.89 us (2%)
    ppermute x11, starting transfers between devices, send(): return lax.ppermute(block, 'seq', route)  14.2 us
    ppermute x11, waiting for transfers between devices, send(): return lax.ppermute(block, 'seq', route)  10.6 us
    pallas_call x4, Pallas kernels, attend(): pl.pallas_call(functools.partial(attend_kernel, sources, later, len(block...  9.35 us
    unnamed x12, local copies, waits for them, and re-layouts  4.4 us
    pallas_call x1, Pallas kernels, pack(): pl.pallas_call(pack_kernel, out_shape=jax.ShapeDtypeStruct((2 * KEY_VALUE...  1.13 us
  transfers between devices with their start and end apart: 11, of which 3 were waited for; matrix products, arithmetic and copies ran while one was open for 0% of the time, Pallas kernels for 21%

profile of v5, /device:TPU:11, one launch (start us, length us, event | category | flops | bytes accessed | tf_op | source)
XLA Modules:
  0.0 40.5 jit_solution(16891213537560059251)
XLA Ops:
  0.6 0.0 copy-start.1
  0.6 1.1 %pack.1.refs_4_ = bf16[8,128,128]{2,1,0:T(8,128)(2,1)S(1)} custom-call(bf16[128,512]{1,0:T(8,128)(2,1)} %keys_ref.1, bf16[128,512]{1,0:T(8,128)(2,1)} %values_ref.1), custom_call_target="tpu_custom_call" | custom-call | tf_op jit(solution)/shard_map/pack/pallas_call | solution.py:69
  1.8 1.3 %collective-permute-start = (bf16[8,128,128]{2,1,0:T(8,128)(2,1)S(1)}, bf16[8,128,128]{2,1,0:T(8,128)(2,1)S(1)}, u32[]{:S(2)}, u32[]{:S(2)}) collective-permute-start(bf16[8,128,128]{2,1,0:T(8,128)(2,1)S(1)} %pack.1.refs_4_), channel_id=1, source_target_pairs={{0,4},{1,5},{2,6},{3,7},{4,8},{5,9},{6,10},{7,11},{8,12},{9,13},{1... | collective-permute-start | bytes 786440 | tf_op jit(solution)/shard_map/ppermute | solution.py:310
  3.1 1.0 %collective-permute-start.10 = (bf16[8,128,128]{2,1,0:T(8,128)(2,1)S(1)}, bf16[8,128,128]{2,1,0:T(8,128)(2,1)S(1)}, u32[]{:S(2)}, u32[]{:S(2)}) collective-permute-start(bf16[8,128,128]{2,1,0:T(8,128)(2,1)S(1)} %pack.1.refs_4_), channel_id=1, source_target_pairs={{0,1},{1,0},{2,3},{3,2},{4,5},{5,4},{6,7},{7,6},{8,9},{9,8},{10,11... | collective-permute-start | bytes 786440 | tf_op jit(solution)/shard_map/ppermute | solution.py:310
  4.1 1.2 %collective-permute-start.7 = (bf16[8,128,128]{2,1,0:T(8,128)(2,1)S(1)}, bf16[8,128,128]{2,1,0:T(8,128)(2,1)S(1)}, u32[]{:S(2)}, u32[]{:S(2)}) collective-permute-start(bf16[8,128,128]{2,1,0:T(8,128)(2,1)S(1)} %pack.1.refs_4_), channel_id=1, source_target_pairs={{0,2},{1,3},{2,0},{3,1},{4,6},{5,7},{6,4},{7,5},{8,10},{9,11},{10,... | collective-permute-start | bytes 786440 | tf_op jit(solution)/shard_map/ppermute | solution.py:310
  5.3 3.7 %collective-permute-done.refs_6_ = bf16[8,128,128]{2,1,0:T(8,128)(2,1)S(1)} collective-permute-done((bf16[8,128,128]{2,1,0:T(8,128)(2,1)S(1)}, bf16[8,128,128]{2,1,0:T(8,128)(2,1)S(1)}, u32[]{:S(2)}, u32[]{:S(2)}) %collective-permute-start) | collective-permute-done | bytes 262176 | tf_op jit(solution)/shard_map/ppermute | solution.py:310
  9.0 1.2 %collective-permute-start.3 = (bf16[8,128,128]{2,1,0:T(8,128)(2,1)S(1)}, bf16[8,128,128]{2,1,0:T(8,128)(2,1)S(1)}, u32[]{:S(2)}, u32[]{:S(2)}) collective-permute-start(bf16[8,128,128]{2,1,0:T(8,128)(2,1)S(1)} %collective-permute-done.refs_6_), channel_id=1, source_target_pairs={{0,2},{1,3},{2,0},{3,1},{4,6},{5,7},{6,4},{7,5},{8,10},{9,11},{10,... | collective-permute-start | bytes 786440 | tf_op jit(solution)/shard_map/ppermute | solution.py:310
  10.3 1.3 %collective-permute-start.5 = (bf16[8,128,128]{2,1,0:T(8,128)(2,1)S(1)}, bf16[8,128,128]{2,1,0:T(8,128)(2,1)S(1)}, u32[]{:S(2)}, u32[]{:S(2)}) collective-permute-start(bf16[8,128,128]{2,1,0:T(8,128)(2,1)S(1)} %collective-permute-done.refs_6_), channel_id=1, source_target_pairs={{0,4},{1,5},{2,6},{3,7},{4,8},{5,9},{6,10},{7,11},{8,12},{9,13},{1... | collective-permute-start | bytes 786440 | tf_op jit(solution)/shard_map/ppermute | solution.py:310
  11.6 0.2 collective-permute-start.1
  11.8 0.0 collective-permute-done.10.refs_5_
  11.8 0.7 %copy-done.4 = bf16[8,128,128]{2,1,0:T(8,128)(2,1)} copy-done((bf16[8,128,128]{2,1,0:T(8,128)(2,1)}, bf16[8,128,128]{2,1,0:T(8,128)(2,1)S(1)}, u32[]{:S(2)}) %copy-start.4) | copy-done | bytes 262168
  12.5 2.4 %collective-permute-start.9 = (bf16[8,128,128]{2,1,0:T(8,128)(2,1)S(1)}, bf16[8,128,128]{2,1,0:T(8,128)(2,1)S(1)}, u32[]{:S(2)}, u32[]{:S(2)}) collective-permute-start(bf16[8,128,128]{2,1,0:T(8,128)(2,1)S(1)} %collective-permute-done.refs_6_), channel_id=1, source_target_pairs={{0,1},{1,0},{2,3},{3,2},{4,5},{5,4},{6,7},{7,6},{8,9},{9,8},{10,11... | collective-permute-start | bytes 786440 | tf_op jit(solution)/shard_map/ppermute | solution.py:310
  14.9 0.0 collective-permute-done.7.refs_4_
  14.9 0.0 collective-permute-start.8
  14.9 1.8 %collective-permute-done.3.refs_4_ = bf16[8,128,128]{2,1,0:T(8,128)(2,1)S(1)} collective-permute-done((bf16[8,128,128]{2,1,0:T(8,128)(2,1)S(1)}, bf16[8,128,128]{2,1,0:T(8,128)(2,1)S(1)}, u32[]{:S(2)}, u32[]{:S(2)}) %collective-permute-start.3) | collective-permute-done | bytes 262176 | tf_op jit(solution)/shard_map/ppermute | solution.py:310
  16.7 2.1 %collective-permute-start.4 = (bf16[8,128,128]{2,1,0:T(8,128)(2,1)S(1)}, bf16[8,128,128]{2,1,0:T(8,128)(2,1)S(1)}, u32[]{:S(2)}, u32[]{:S(2)}) collective-permute-start(bf16[8,128,128]{2,1,0:T(8,128)(2,1)S(1)} %collective-permute-done.3.refs_4_), channel_id=1, source_target_pairs={{0,1},{1,0},{2,3},{3,2},{4,5},{5,4},{6,7},{7,6},{8,9},{9,8},{10,11... | collective-permute-start | bytes 786440 | tf_op jit(solution)/shard_map/ppermute | solution.py:310
  18.8 0.0 collective-permute-done.5.refs_6_
  18.8 0.8 %collective-permute-start.6 = (bf16[8,128,128]{2,1,0:T(8,128)(2,1)S(1)}, bf16[8,128,128]{2,1,0:T(8,128)(2,1)S(1)}, u32[]{:S(2)}, u32[]{:S(2)}) collective-permute-start(bf16[8,128,128]{2,1,0:T(8,128)(2,1)S(1)} %collective-permute-done.5.refs_6_), channel_id=1, source_target_pairs={{0,1},{1,0},{2,3},{3,2},{4,5},{5,4},{6,7},{7,6},{8,9},{9,8},{10,11... | collective-permute-start | bytes 786440 | tf_op jit(solution)/shard_map/ppermute | solution.py:310
  19.6 5.0 %collective-permute-done.1.refs_4_ = bf16[8,128,128]{2,1,0:T(8,128)(2,1)S(1)} collective-permute-done((bf16[8,128,128]{2,1,0:T(8,128)(2,1)S(1)}, bf16[8,128,128]{2,1,0:T(8,128)(2,1)S(1)}, u32[]{:S(2)}, u32[]{:S(2)}) %collective-permute-start.1) | collective-permute-done | bytes 262176 | tf_op jit(solution)/shard_map/ppermute | solution.py:310
  24.6 2.6 %collective-permute-start.2 = (bf16[8,128,128]{2,1,0:T(8,128)(2,1)S(1)}, bf16[8,128,128]{2,1,0:T(8,128)(2,1)S(1)}, u32[]{:S(2)}, u32[]{:S(2)}) collective-permute-start(bf16[8,128,128]{2,1,0:T(8,128)(2,1)S(1)} %collective-permute-done.1.refs_4_), channel_id=1, source_target_pairs={{0,1},{1,0},{2,3},{3,2},{4,5},{5,4},{6,7},{7,6},{8,9},{9,8},{10,11... | collective-permute-start | bytes 786440 | tf_op jit(solution)/shard_map/ppermute | solution.py:310
  27.3 1.0 %copy-done = bf16[128,2048]{1,0:T(8,128)(2,1)S(1)} copy-done((bf16[128,2048]{1,0:T(8,128)(2,1)S(1)}, bf16[128,2048]{1,0:T(8,128)(2,1)}, u32[]{:S(2)}) %copy-start) | copy-done | bytes 524312
  28.3 1.0 %copy-done.2 = bf16[128,2048]{1,0:T(8,128)(2,1)S(1)} copy-done((bf16[128,2048]{1,0:T(8,128)(2,1)S(1)}, bf16[128,2048]{1,0:T(8,128)(2,1)}, u32[]{:S(2)}) %copy-start.2) | copy-done | bytes 524312
  29.3 0.7 %copy-done.3 = s32[4]{0:T(128)S(1)} copy-done((s32[4]{0:T(128)S(1)}, s32[4]{0:T(128)}, u32[]{:S(2)}) %copy-start.3) | copy-done | bytes 40
  30.0 0.9 %copy-done.5 = bf16[8,128,128]{2,1,0:T(8,128)(2,1)S(1)} copy-done((bf16[8,128,128]{2,1,0:T(8,128)(2,1)S(1)}, bf16[8,128,128]{2,1,0:T(8,128)(2,1)}, u32[]{:S(2)}) %copy-start.5) | copy-done | bytes 262168
  30.9 2.0 %attend.3 = (f32[16,128,256]{2,1,0:T(8,128)S(1)}, f32[32,256]{1,0:T(8,128)S(1)}) custom-call(s32[1]{0:T(128)} %bitcast.refs_0_, s32[4]{0:T(128)S(1)} %copy-done.3, bf16[128,2048]{1,0:T(8,128)(2,1)S(1)} %copy-done, bf16[128,2048]{1,0:T(8,128)(2,1)S(1)} %copy-done.2, bf16[8,128,128]{2,1,0:T(8,128)(2,1)S(1)} %pack.1.refs_4_, bf16[8,128,128]{2,1,0:T(8,128)(2,1)S(1)} %copy-done.5), custom_call_target="tpu_custom_call" | custom-call | flops 536870912 | bytes 1572864 | tf_op jit(solution)/shard_map/attend/pallas_call | solution.py:284
  33.0 0.0 collective-permute-done.9.refs_7_
  33.0 0.0 collective-permute-done.8.refs_5_
  33.0 2.6 %attend.4 = (f32[16,128,256]{2,1,0:T(8,128)S(1)}, f32[32,256]{1,0:T(8,128)S(1)}) custom-call(s32[1]{0:T(128)} %bitcast.refs_0_, s32[4]{0:T(128)S(1)} %copy-done.3, bf16[128,2048]{1,0:T(8,128)(2,1)S(1)} %copy-done.1, bf16[128,2048]{1,0:T(8,128)(2,1)S(1)} %copy-done.2, ...), custom_call_target="tpu_custom_call", output_to_operand_aliasing={{0}: (8, {}), {1}: (9, {})} | custom-call | flops 1073741824 | bytes 2097152 | tf_op jit(solution)/shard_map/attend/pallas_call | solution.py:284
  35.6 0.0 collective-permute-done.4.refs_5_
  35.7 4.0 %attend.5 = (f32[16,128,256]{2,1,0:T(8,128)S(1)}, f32[32,256]{1,0:T(8,128)S(1)}, bf16[128,2048]{1,0:T(8,128)(2,1)}, bf16[128,2048]{1,0:T(8,128)(2,1)}) custom-call(s32[1]{0:T(128)} %bitcast.refs_0_, s32[4]{0:T(128)S(1)} %copy-done.3, bf16[128,2048]{1,0:T(8,128)(2,1)S(1)} %copy-done.1, ...), custom_call_target="tpu_custom_call", output_to_operand_aliasing={{0}: (8, {}), {1}: (9, {})} | custom-call | flops 1073741824 | bytes 2097152 | tf_op jit(solution)/shard_map/attend/pallas_call | solution.py:284
  39.7 0.0 collective-permute-done.2.refs_5_
  39.7 0.7 %attend_last.1 = (bf16[128,2048]{1,0:T(8,128)(2,1)}, bf16[128,2048]{1,0:T(8,128)(2,1)}) custom-call(s32[1]{0:T(128)} %bitcast.refs_0_, s32[4]{0:T(128)S(1)} %copy-done.3, bf16[128,2048]{1,0:T(8,128)(2,1)S(1)} %copy-done.1, bf16[128,2048]{1,0:T(8,128)(2,1)S(1)} %copy-done.2, ...), custom_call_target="tpu_custom_call", output_to_operand_aliasing={{0}: (8, {}), {1}: (9, {})} | custom-call | flops 536870912 | bytes 1572864 | tf_op jit(solution)/shard_map/attend_last/pallas_call | solution.py:284
  (7 shorter events, 0.0 us)
Async XLA Ops:
  0.6 32.4 %copy-start.1 = (bf16[128,2048]{1,0:T(8,128)(2,1)S(1)}, bf16[128,2048]{1,0:T(8,128)(2,1)}, u32[]{:S(2)}) copy-start(bf16[128,2048]{1,0:T(8,128)(2,1)} %refs_2_.7) | copy-start | bytes 1572868
  1.8 7.2 %collective-permute-start = (bf16[8,128,128]{2,1,0:T(8,128)(2,1)S(1)}, bf16[8,128,128]{2,1,0:T(8,128)(2,1)S(1)}, u32[]{:S(2)}, u32[]{:S(2)}) collective-permute-start(bf16[8,128,128]{2,1,0:T(8,128)(2,1)S(1)} %pack.1.refs_4_), channel_id=1, source_target_pairs={{0,4},{1,5},{2,6},{3,7},{4,8},{5,9},{6,10},{7,11},{8,12},{9,13},{1... | collective-permute-start | bytes 786440 | tf_op jit(solution)/shard_map/ppermute | solution.py:310
  3.1 8.7 %collective-permute-start.10 = (bf16[8,128,128]{2,1,0:T(8,128)(2,1)S(1)}, bf16[8,128,128]{2,1,0:T(8,128)(2,1)S(1)}, u32[]{:S(2)}, u32[]{:S(2)}) collective-permute-start(bf16[8,128,128]{2,1,0:T(8,128)(2,1)S(1)} %pack.1.refs_4_), channel_id=1, source_target_pairs={{0,1},{1,0},{2,3},{3,2},{4,5},{5,4},{6,7},{7,6},{8,9},{9,8},{10,11... | collective-permute-start | bytes 786440 | tf_op jit(solution)/shard_map/ppermute | solution.py:310
  4.1 10.8 %collective-permute-start.7 = (bf16[8,128,128]{2,1,0:T(8,128)(2,1)S(1)}, bf16[8,128,128]{2,1,0:T(8,128)(2,1)S(1)}, u32[]{:S(2)}, u32[]{:S(2)}) collective-permute-start(bf16[8,128,128]{2,1,0:T(8,128)(2,1)S(1)} %pack.1.refs_4_), channel_id=1, source_target_pairs={{0,2},{1,3},{2,0},{3,1},{4,6},{5,7},{6,4},{7,5},{8,10},{9,11},{10,... | collective-permute-start | bytes 786440 | tf_op jit(solution)/shard_map/ppermute | solution.py:310
  9.0 7.7 %collective-permute-start.3 = (bf16[8,128,128]{2,1,0:T(8,128)(2,1)S(1)}, bf16[8,128,128]{2,1,0:T(8,128)(2,1)S(1)}, u32[]{:S(2)}, u32[]{:S(2)}) collective-permute-start(bf16[8,128,128]{2,1,0:T(8,128)(2,1)S(1)} %collective-permute-done.refs_6_), channel_id=1, source_target_pairs={{0,2},{1,3},{2,0},{3,1},{4,6},{5,7},{6,4},{7,5},{8,10},{9,11},{10,... | collective-permute-start | bytes 786440 | tf_op jit(solution)/shard_map/ppermute | solution.py:310
  10.3 8.5 %collective-permute-start.5 = (bf16[8,128,128]{2,1,0:T(8,128)(2,1)S(1)}, bf16[8,128,128]{2,1,0:T(8,128)(2,1)S(1)}, u32[]{:S(2)}, u32[]{:S(2)}) collective-permute-start(bf16[8,128,128]{2,1,0:T(8,128)(2,1)S(1)} %collective-permute-done.refs_6_), channel_id=1, source_target_pairs={{0,4},{1,5},{2,6},{3,7},{4,8},{5,9},{6,10},{7,11},{8,12},{9,13},{1... | collective-permute-start | bytes 786440 | tf_op jit(solution)/shard_map/ppermute | solution.py:310
  11.6 13.1 %collective-permute-start.1 = (bf16[8,128,128]{2,1,0:T(8,128)(2,1)S(1)}, bf16[8,128,128]{2,1,0:T(8,128)(2,1)S(1)}, u32[]{:S(2)}, u32[]{:S(2)}) collective-permute-start(bf16[8,128,128]{2,1,0:T(8,128)(2,1)S(1)} %collective-permute-done.refs_6_), channel_id=1, source_target_pairs={{0,2},{1,3},{2,0},{3,1},{4,6},{5,7},{6,8},{7,9},{8,10},{9,11},{10,... | collective-permute-start | bytes 786440 | tf_op jit(solution)/shard_map/ppermute | solution.py:310
  11.8 0.7 %copy-start.4 = (bf16[8,128,128]{2,1,0:T(8,128)(2,1)}, bf16[8,128,128]{2,1,0:T(8,128)(2,1)S(1)}, u32[]{:S(2)}) copy-start(bf16[8,128,128]{2,1,0:T(8,128)(2,1)S(1)} %collective-permute-done.10.refs_5_) | copy-start | bytes 786436
  12.5 20.5 %collective-permute-start.9 = (bf16[8,128,128]{2,1,0:T(8,128)(2,1)S(1)}, bf16[8,128,128]{2,1,0:T(8,128)(2,1)S(1)}, u32[]{:S(2)}, u32[]{:S(2)}) collective-permute-start(bf16[8,128,128]{2,1,0:T(8,128)(2,1)S(1)} %collective-permute-done.refs_6_), channel_id=1, source_target_pairs={{0,1},{1,0},{2,3},{3,2},{4,5},{5,4},{6,7},{7,6},{8,9},{9,8},{10,11... | collective-permute-start | bytes 786440 | tf_op jit(solution)/shard_map/ppermute | solution.py:310
  14.9 18.1 %collective-permute-start.8 = (bf16[8,128,128]{2,1,0:T(8,128)(2,1)S(1)}, bf16[8,128,128]{2,1,0:T(8,128)(2,1)S(1)}, u32[]{:S(2)}, u32[]{:S(2)}) collective-permute-start(bf16[8,128,128]{2,1,0:T(8,128)(2,1)S(1)} %collective-permute-done.7.refs_4_), channel_id=1, source_target_pairs={{0,1},{1,0},{2,3},{3,2},{4,5},{5,4},{6,7},{7,6},{8,9},{9,8},{10,11... | collective-permute-start | bytes 786440 | tf_op jit(solution)/shard_map/ppermute | solution.py:310
  16.7 18.9 %collective-permute-start.4 = (bf16[8,128,128]{2,1,0:T(8,128)(2,1)S(1)}, bf16[8,128,128]{2,1,0:T(8,128)(2,1)S(1)}, u32[]{:S(2)}, u32[]{:S(2)}) collective-permute-start(bf16[8,128,128]{2,1,0:T(8,128)(2,1)S(1)} %collective-permute-done.3.refs_4_), channel_id=1, source_target_pairs={{0,1},{1,0},{2,3},{3,2},{4,5},{5,4},{6,7},{7,6},{8,9},{9,8},{10,11... | collective-permute-start | bytes 786440 | tf_op jit(solution)/shard_map/ppermute | solution.py:310
  18.8 16.9 %collective-permute-start.6 = (bf16[8,128,128]{2,1,0:T(8,128)(2,1)S(1)}, bf16[8,128,128]{2,1,0:T(8,128)(2,1)S(1)}, u32[]{:S(2)}, u32[]{:S(2)}) collective-permute-start(bf16[8,128,128]{2,1,0:T(8,128)(2,1)S(1)} %collective-permute-done.5.refs_6_), channel_id=1, source_target_pairs={{0,1},{1,0},{2,3},{3,2},{4,5},{5,4},{6,7},{7,6},{8,9},{9,8},{10,11... | collective-permute-start | bytes 786440 | tf_op jit(solution)/shard_map/ppermute | solution.py:310
  24.6 15.0 %collective-permute-start.2 = (bf16[8,128,128]{2,1,0:T(8,128)(2,1)S(1)}, bf16[8,128,128]{2,1,0:T(8,128)(2,1)S(1)}, u32[]{:S(2)}, u32[]{:S(2)}) collective-permute-start(bf16[8,128,128]{2,1,0:T(8,128)(2,1)S(1)} %collective-permute-done.1.refs_4_), channel_id=1, source_target_pairs={{0,1},{1,0},{2,3},{3,2},{4,5},{5,4},{6,7},{7,6},{8,9},{9,8},{10,11... | collective-permute-start | bytes 786440 | tf_op jit(solution)/shard_map/ppermute | solution.py:310
  27.3 1.0 %copy-start = (bf16[128,2048]{1,0:T(8,128)(2,1)S(1)}, bf16[128,2048]{1,0:T(8,128)(2,1)}, u32[]{:S(2)}) copy-start(bf16[128,2048]{1,0:T(8,128)(2,1)} %refs_2_.7) | copy-start | bytes 1572868
  28.3 1.0 %copy-start.2 = (bf16[128,2048]{1,0:T(8,128)(2,1)S(1)}, bf16[128,2048]{1,0:T(8,128)(2,1)}, u32[]{:S(2)}) copy-start(bf16[128,2048]{1,0:T(8,128)(2,1)} %refs_3_.7) | copy-start | bytes 1572868
  29.3 0.7 %copy-start.3 = (s32[4]{0:T(128)S(1)}, s32[4]{0:T(128)}, u32[]{:S(2)}) copy-start(s32[4]{0:T(128)} %refs_1_.7) | copy-start | bytes 52
  30.0 0.9 %copy-start.5 = (bf16[8,128,128]{2,1,0:T(8,128)(2,1)S(1)}, bf16[8,128,128]{2,1,0:T(8,128)(2,1)}, u32[]{:S(2)}) copy-start(bf16[8,128,128]{2,1,0:T(8,128)(2,1)} %copy-done.4) | copy-start | bytes 786436
